TPU v7x, 256 devices: a whole 4x4x8 slice. The times are simulated.
256 devices in a mesh: row: 8 (over z), col: 32 (over y, x, core).
Axes of the slice: x: 4, y: 4, z: 8, core: 2. Of those that a mesh axis runs over, the one named last changes fastest.
Arguments:
- node_latent: bfloat16 [262144, 128], P(('row', 'col')), may hold values from -6 to 6
- edge_latent: bfloat16 [1048576, 128], P(('row', 'col')), may hold values from -6 to 6
- senders: int32 [1048576], P(('row', 'col')), may hold values from 0 to 1535
- receivers: int32 [1048576], P(('row', 'col')), may hold values from 0 to 1023
- send_index: int32 [256, 4, 128], P(('row', 'col')), may hold values from 0 to 1023
- context_table: bfloat16 [2048, 128], P(('row', 'col')), may hold values from -6 to 6
- region: int32 [262144], P(('row', 'col')), may hold values from 0 to 2047
- edge_w1: bfloat16 [2, 384, 128], replicated, may hold values from -0.3125 to 0.3125
- edge_w2: bfloat16 [2, 128, 128], replicated, may hold values from -0.5 to 0.5
- edge_bias: float32 [2, 3, 128], replicated, may hold values from -3 to 3
- edge_gain: float32 [2, 128], replicated, may hold values from 0.25 to 1.75
- node_w1: bfloat16 [2, 384, 128], replicated, may hold values from -0.3125 to 0.3125
- node_wg: bfloat16 [2, 128, 128], replicated, may hold values from -0.5 to 0.5
- node_w2: bfloat16 [2, 128, 128], replicated, may hold values from -0.5 to 0.5
- node_bias: float32 [2, 3, 128], replicated, may hold values from -3 to 3
- node_gain: float32 [2, 128], replicated, may hold values from 0.25 to 1.75
Outputs:
- node_out: bfloat16 [262144, 128], P(('row', 'col'))
- edge_out: bfloat16 [1048576, 128], P(('row', 'col'))
Inputs may be any that keep to these rules, and one draw needn't show every extreme that they name: senders index the extended table of the edge's own partition: below 1024 its own nodes, then the four received blocks of 128 rows in the order above, below, left, right. receivers are nodes of the edge's own partition. `send_index`: rows of the sending partition's own nodes; repeats may occur.
All inputs are finite; a program needn't handle non-finite values.
Results may differ from a plain program's by a relative error of at most 0.0085.
Values may be sent and summed in bfloat16 or wider, within the bound.
No kernel may reach another device: no remote copies, remote signals or barrier semaphores. Data moves between devices by JAX's collectives and lax.ppermute only.
A program may use at most 64 MiB of HBM per device.

v0:
```python
import functools
import math

import jax
import jax.numpy as jnp
from jax import lax
from jax.sharding import Mesh
from jax.sharding import PartitionSpec as P

LAYERS = 2
COL = ("col_0", "col_1", "col_2")
ROW_COL = ("row", "col_0", "col_1", "col_2")


EPS = 1e-05


def passed_along(value, axis, by):
    devices = lax.axis_size(axis)
    pairs = [(i, i + by) for i in range(devices) if 0 <= i + by < devices]
    return lax.ppermute(value, axis, pairs)


def one_axis_at_a_time(value, axes):
    return functools.reduce(lax.psum, axes, value)


def in_order(pieces, dim):
    shape = list(pieces.shape[1:])
    shape[dim] *= pieces.shape[0]
    return jnp.moveaxis(pieces, 0, dim).reshape(shape)


def from_everyone(value, axis):
    copies = jnp.broadcast_to(value, (lax.axis_size(axis), *value.shape))
    return lax.all_to_all(copies, axis, split_axis=0, concat_axis=0, tiled=True)


def gathered_copies(value, axis, dim):
    return in_order(from_everyone(value, axis), dim)


def norm_tail(pre, w_out, b_out, gain, shift):
    hidden = jax.nn.relu(pre).astype(jnp.bfloat16)
    y_val = jnp.dot(hidden, w_out, preferred_element_type=jnp.float32) + b_out
    centred = y_val - jnp.mean(y_val, axis=-1, keepdims=True)
    spread = jnp.mean(centred * centred, axis=-1, keepdims=True)
    return centred * lax.rsqrt(spread + EPS) * gain + shift


def one_hot(index, count):
    columns = lax.broadcasted_iota(jnp.int32, (1, count), 1)
    return (index[:, None] == columns).astype(jnp.bfloat16)


def lookup(index, table):
    picker = one_hot(index, table.shape[0])
    return jnp.dot(picker, table, preferred_element_type=jnp.float32).astype(jnp.bfloat16)


def blocked_lookup(index, table):
    total_rows = index.shape[0]
    block_rows = math.gcd(total_rows, 512)
    pieces = index.reshape(total_rows // block_rows, block_rows)
    result = lax.map(lambda piece: lookup(piece, table), pieces)
    return result.reshape(total_rows, table.shape[1])


def edge_and_sum(extended, nodes, edges, senders, receivers, w_in, w_out, bias, gain):
    total_rows = edges.shape[0]
    width = edges.shape[1]
    node_count = nodes.shape[0]
    block_rows = math.gcd(total_rows, 512)
    blocks = total_rows // block_rows

    def one_block(summed, items):
        edge_rows, send_rows, recv_rows = items
        recv_hot = one_hot(recv_rows, node_count)
        sender_feats = lookup(send_rows, extended)
        receiver_feats = jnp.dot(recv_hot, nodes, preferred_element_type=jnp.float32).astype(
            jnp.bfloat16
        )
        feats = jnp.concatenate([sender_feats, receiver_feats, edge_rows], axis=1)
        pre = jnp.dot(feats, w_in, preferred_element_type=jnp.float32) + bias[0]
        fresh = (
            edge_rows.astype(jnp.float32) + norm_tail(pre, w_out, bias[1], gain, bias[2])
        ).astype(jnp.bfloat16)
        added = lax.dot_general(
            recv_hot, fresh, (((0,), (0,)), ((), ())), preferred_element_type=jnp.float32
        )
        return (summed + added, fresh)

    start = jnp.zeros((node_count, width), jnp.float32)
    items = (
        edges.reshape(blocks, block_rows, width),
        senders.reshape(blocks, block_rows),
        receivers.reshape(blocks, block_rows),
    )
    summed, fresh = lax.scan(one_block, start, items)
    return (fresh.reshape(total_rows, width), summed.astype(jnp.bfloat16))


def node_step(nodes, summed, context_rows, w_in, w_out, bias, gain, shift_in):
    feats = jnp.concatenate([nodes, summed, context_rows], axis=1)
    pre = jnp.dot(feats, w_in, preferred_element_type=jnp.float32) + shift_in
    return (nodes.astype(jnp.float32) + norm_tail(pre, w_out, bias[1], gain, bias[2])).astype(
        jnp.bfloat16
    )


def row_move(block, offset):
    return passed_along(block, "row", offset)


def col_move(block, offset):
    return passed_along(block, COL, offset)


def extend(nodes, send_index):
    count = send_index.shape[2]
    width = nodes.shape[1]
    picked = lookup(send_index.reshape(-1), nodes).reshape(4, count, width)
    return jnp.concatenate(
        [
            nodes,
            row_move(picked[0], 1),
            row_move(picked[1], -1),
            col_move(picked[2], 1),
            col_move(picked[3], -1),
        ],
        axis=0,
    )


def local(
    node_latent,
    edge_latent,
    senders,
    receivers,
    send_index,
    context_table,
    region,
    edge_w1,
    edge_w2,
    edge_bias,
    edge_gain,
    node_w1,
    node_wg,
    node_w2,
    node_bias,
    node_gain,
):
    width = node_latent.shape[1]
    local_sum = jnp.sum(node_latent.astype(jnp.float32), axis=0)
    total = one_axis_at_a_time(local_sum, ROW_COL)
    by_row = gathered_copies(context_table[None], "row", 0)
    table = gathered_copies(by_row, COL, 1).reshape(-1, width)
    node_count = node_latent.shape[0] * lax.axis_size("row") * lax.axis_size(COL)
    pooled = total / math.sqrt(node_count)
    context_rows = blocked_lookup(region, table)
    nodes = node_latent
    edges = edge_latent
    for layer in range(LAYERS):
        extended = extend(nodes, send_index)
        edges, summed = edge_and_sum(
            extended,
            nodes,
            edges,
            senders,
            receivers,
            edge_w1[layer],
            edge_w2[layer],
            edge_bias[layer],
            edge_gain[layer],
        )
        shift_in = node_bias[layer, 0] + jnp.dot(pooled, node_wg[layer].astype(jnp.float32))
        nodes = node_step(
            nodes,
            summed,
            context_rows,
            node_w1[layer],
            node_w2[layer],
            node_bias[layer],
            node_gain[layer],
            shift_in,
        )
    return (nodes, edges)


def solution(mesh):
    finer = Mesh(
        mesh.devices.reshape(mesh.shape["row"], 4, 4, 2), ("row", "col_0", "col_1", "col_2")
    )
    placed = (
        P(ROW_COL, None),
        P(ROW_COL, None),
        P(ROW_COL),
        P(ROW_COL),
        P(ROW_COL, None, None),
        P(ROW_COL, None),
        P(ROW_COL),
        P(),
        P(),
        P(),
        P(),
        P(),
        P(),
        P(),
        P(),
        P(),
    )
    return jax.shard_map(
        local,
        mesh=finer,
        in_specs=placed,
        out_specs=(P(ROW_COL, None), P(ROW_COL, None)),
        check_vma=False,
    )
```

profile of v0, /device:TPU:39, one launch (start us, length us, event | category | flops | bytes accessed | tf_op | source)
XLA Modules:
  0.0 207.6 jit_solution(10631488229100498402)
XLA Ops:
  0.7 1.5 fusion.63
  2.9 3.7 %collective-permute-start = (bf16[128,128]{1,0:T(8,128)(2,1)}, bf16[128,128]{1,0:T(8,128)(2,1)}, u32[]{:S(2)}, u32[]{:S(2)}) collective-permute-start(bf16[128,128]{1,0:T(8,128)(2,1)} %get-tuple-element.408), channel_id=1, source_target_pairs={{0,32},{32,64},{64,96},{96,128},{128,160},{160,192},{192,224},{1,3... | collective-permute-start | bytes 98312 | tf_op jit(solution)/shard_map/ppermute | solution.py:21
  6.6 2.3 %collective-permute-start.1 = (bf16[128,128]{1,0:T(8,128)(2,1)}, bf16[128,128]{1,0:T(8,128)(2,1)}, u32[]{:S(2)}, u32[]{:S(2)}) collective-permute-start(bf16[128,128]{1,0:T(8,128)(2,1)} %get-tuple-element.407), channel_id=1, source_target_pairs={{32,0},{64,32},{96,64},{128,96},{160,128},{192,160},{224,192},{33,... | collective-permute-start | bytes 98312 | tf_op jit(solution)/shard_map/ppermute | solution.py:21
  8.9 4.2 %collective-permute-start.2 = (bf16[128,128]{1,0:T(8,128)(2,1)}, bf16[128,128]{1,0:T(8,128)(2,1)}, u32[]{:S(2)}, u32[]{:S(2)}) collective-permute-start(bf16[128,128]{1,0:T(8,128)(2,1)} %get-tuple-element.406), channel_id=1, source_target_pairs={{0,1},{1,2},{2,3},{3,4},{4,5},{5,6},{6,7},{7,8},{8,9},{9,10},{10,1... | collective-permute-start | bytes 98312 | tf_op jit(solution)/shard_map/ppermute | solution.py:21
  13.2 1.9 collective-permute-start.3
  15.7 8.6 %all-to-all-start = ((bf16[8,1,8,128]{3,2,1,0:T(8,128)(2,1)}), bf16[8,1,8,128]{3,2,1,0:T(8,128)(2,1)S(1)}, u32[]{:S(2)}, u32[]{:S(2)}) async-start(bf16[8,1,8,128]{3,2,1,0:T(8,128)(2,1)} %broadcast_in_dim.23), calls=%async_computation | async-start | bytes 32768 | tf_op jit(solution)/shard_map/all_to_all | solution.py:36
  27.1 11.9 %psum.28 = f32[128]{0:T(128)S(1)} all-reduce(f32[128]{0:T(128)S(1)} %convert_reduce_fusion), channel_id=1, replica_groups=mesh['row'=8,'col_0'=4,'col_1'=4,'col_2'=2] {'row'}, use_global_device_ids=true, to_apply=%region_7.8 | all-reduce | flops 128 | bytes 1024 | tf_op jit(solution)/shard_map/psum | solution.py:25
  39.0 7.9 %psum.29 = f32[128]{0:T(128)S(1)} all-reduce(f32[128]{0:T(128)S(1)} %psum.28), channel_id=1, replica_groups=mesh['row'=8,'col_0'=4,'col_1'=4,'col_2'=2] {'col_0'}, use_global_device_ids=true, to_apply=%region_8.9 | all-reduce | flops 128 | bytes 1024 | tf_op jit(solution)/shard_map/psum | solution.py:25
  46.9 6.1 %psum.30 = f32[128]{0:T(128)S(1)} all-reduce(f32[128]{0:T(128)S(1)} %psum.29), channel_id=1, replica_groups=mesh['row'=8,'col_0'=4,'col_1'=4,'col_2'=2] {'col_1'}, use_global_device_ids=true, to_apply=%region_9.10 | all-reduce | flops 128 | bytes 1024 | tf_op jit(solution)/shard_map/psum | solution.py:25
  52.9 12.9 %psum.31 = f32[128]{0:T(128)S(1)} all-reduce(f32[128]{0:T(128)S(1)} %psum.30), channel_id=1, replica_groups=mesh['row'=8,'col_0'=4,'col_1'=4,'col_2'=2] {'col_2'}, use_global_device_ids=true, to_apply=%region_10.11 | all-reduce | flops 128 | bytes 1024 | tf_op jit(solution)/shard_map/psum | solution.py:25
  68.8 5.4 %all-to-all-start.1 = ((bf16[32,8,8,128]{3,2,1,0:T(8,128)(2,1)}), bf16[32,8,8,128]{3,2,1,0:T(8,128)(2,1)S(1)}, u32[]{:S(2)}, u32[]{:S(2)}) async-start(bf16[32,8,8,128]{3,2,1,0:T(8,128)(2,1)} %broadcast_in_dim.24), calls=%async_computation.1 | async-start | bytes 1048576 | tf_op jit(solution)/shard_map/all_to_all | solution.py:36
  76.5 57.4 %while.37 = (s32[]{:T(128)}, f32[1024,128]{1,0:T(8,128)S(1)}, bf16[8,512,128]{1,2,0:T(8,128)(2,1)S(1)}, s32[8,512]{1,0:T(8,128)S(1)}, bf16[8,512,128]{2,1,0:T(8,...) while((s32[]{:T(128)}, f32[1024,128]{1,0:T(8,128)S(1)}, ...), condition=%wide.region_3.0_spmd.clone, body=%wide.region_0.3_spmd.clone.sunk | while | flops 541786624 | bytes 7509203 | solution.py:99
  77.8 1.5 fusion.178
  80.4 1.5 fusion.179
  85.0 1.5 fusion.178
  92.2 1.5 fusion.178
  99.3 1.5 fusion.178
  101.9 1.5 fusion.179
  106.5 1.5 fusion.178
  109.1 1.5 fusion.179
  113.7 1.5 fusion.178
  116.3 1.5 fusion.179
  120.9 1.5 fusion.178
  123.4 1.5 fusion.179
  128.0 1.5 fusion.178
  134.2 1.9 while.36
  138.3 2.3 %collective-permute-start.4 = (bf16[128,128]{0,1:T(8,128)(2,1)S(1)}, bf16[128,128]{0,1:T(8,128)(2,1)S(1)}, u32[]{:S(2)}, u32[]{:S(2)}) collective-permute-start(bf16[128,128]{0,1:T(8,128)(2,1)S(1)} %get-tuple-element.404), channel_id=1, source_target_pairs={{0,32},{32,64},{64,96},{96,128},{128,160},{160,192},{192,224},{1,3... | collective-permute-start | bytes 98312 | tf_op jit(solution)/shard_map/ppermute | solution.py:21
  141.6 3.0 %collective-permute-start.5 = (bf16[128,128]{0,1:T(8,128)(2,1)S(1)}, bf16[128,128]{0,1:T(8,128)(2,1)S(1)}, u32[]{:S(2)}, u32[]{:S(2)}) collective-permute-start(bf16[128,128]{0,1:T(8,128)(2,1)S(1)} %get-tuple-element.403), channel_id=1, source_target_pairs={{32,0},{64,32},{96,64},{128,96},{160,128},{192,160},{224,192},{33,... | collective-permute-start | bytes 98312 | tf_op jit(solution)/shard_map/ppermute | solution.py:21
  144.6 3.9 %collective-permute-start.6 = (bf16[128,128]{0,1:T(8,128)(2,1)S(1)}, bf16[128,128]{0,1:T(8,128)(2,1)S(1)}, u32[]{:S(2)}, u32[]{:S(2)}) collective-permute-start(bf16[128,128]{0,1:T(8,128)(2,1)S(1)} %get-tuple-element.402), channel_id=1, source_target_pairs={{0,1},{1,2},{2,3},{3,4},{4,5},{5,6},{6,7},{7,8},{8,9},{9,10},{10,1... | collective-permute-start | bytes 98312 | tf_op jit(solution)/shard_map/ppermute | solution.py:21
  148.5 2.1 %collective-permute-start.7 = (bf16[128,128]{0,1:T(8,128)(2,1)S(1)}, bf16[128,128]{0,1:T(8,128)(2,1)S(1)}, u32[]{:S(2)}, u32[]{:S(2)}) collective-permute-start(bf16[128,128]{0,1:T(8,128)(2,1)S(1)} %get-tuple-element.401), channel_id=1, source_target_pairs={{1,0},{2,1},{3,2},{4,3},{5,4},{6,5},{7,6},{8,7},{9,8},{10,9},{11,1... | collective-permute-start | bytes 98312 | tf_op jit(solution)/shard_map/ppermute | solution.py:21
  150.7 5.1 %collective-permute-done.7 = bf16[128,128]{0,1:T(8,128)(2,1)S(1)} collective-permute-done((bf16[128,128]{0,1:T(8,128)(2,1)S(1)}, bf16[128,128]{0,1:T(8,128)(2,1)S(1)}, u32[]{:S(2)}, u32[]{:S(2)}) %collective-permute-start.7) | collective-permute-done | bytes 32800 | tf_op jit(solution)/shard_map/ppermute | solution.py:21
  156.1 48.7 %while.38 = (s32[]{:T(128)}, f32[1024,128]{1,0:T(8,128)S(1)}, bf16[8,512,128]{2,1,0:T(8,128)(2,1)}, s32[8,512]{1,0:T(8,128)S(1)}, bf16[8,512,128]{1,2,0:T(8,128)...) while((s32[]{:T(128)}, f32[1024,128]{1,0:T(8,128)S(1)}, ...), condition=%wide.region_16.17_spmd.clone, body=%wide.region_13.16_spmd.clone.sunk | while | flops 541786624 | bytes 4626103 | solution.py:99
  (355 shorter events, 102.6 us)
Async XLA Ops:
  0.6 23.7 %copy-start = (bf16[1024,128]{1,0:T(8,128)(2,1)S(1)}, bf16[1024,128]{1,0:T(8,128)(2,1)}, u32[]{:S(2)}) copy-start(bf16[1024,128]{1,0:T(8,128)(2,1)} %param.22) | copy-start | bytes 786436
  0.6 14.4 %copy-start.16 = (bf16[8,128]{1,0:T(8,128)(2,1)S(1)}, bf16[8,128]{1,0:T(8,128)(2,1)}, u32[]{:S(2)}) copy-start(bf16[8,128]{1,0:T(8,128)(2,1)} %param.27) | copy-start | bytes 6148
  0.7 23.9 %copy-start.1 = (bf16[2,384,128]{2,1,0:T(8,128)(2,1)S(1)}, bf16[2,384,128]{2,1,0:T(8,128)(2,1)}, u32[]{:S(2)}) copy-start(bf16[2,384,128]{2,1,0:T(8,128)(2,1)} %param.29) | copy-start | bytes 589828
  0.7 24.5 %copy-start.4 = (bf16[2,128,128]{2,1,0:T(8,128)(2,1)S(1)}, bf16[2,128,128]{2,1,0:T(8,128)(2,1)}, u32[]{:S(2)}) copy-start(bf16[2,128,128]{2,1,0:T(8,128)(2,1)} %param.30) | copy-start | bytes 196612
  0.7 25.1 %copy-start.11 = (f32[2,3,128]{2,0,1:T(2,128)S(1)}, f32[2,3,128]{2,0,1:T(2,128)}, u32[]{:S(2)}) copy-start(f32[2,3,128]{2,0,1:T(2,128)} %param.31) | copy-start | bytes 9220
  0.7 25.7 %copy-start.18 = (f32[2,128]{1,0:T(2,128)S(1)}, f32[2,128]{1,0:T(2,128)}, u32[]{:S(2)}) copy-start(f32[2,128]{1,0:T(2,128)} %param.32) | copy-start | bytes 3076
  2.2 63.6 %copy-start.17 = (f32[2,3,128]{2,0,1:T(2,128)S(1)}, f32[2,3,128]{2,0,1:T(2,128)}, u32[]{:S(2)}) copy-start(f32[2,3,128]{2,0,1:T(2,128)} %param.36) | copy-start | bytes 9220
  2.2 64.2 %copy-start.19 = (f32[2,128]{1,0:T(2,128)S(1)}, f32[2,128]{1,0:T(2,128)}, u32[]{:S(2)}) copy-start(f32[2,128]{1,0:T(2,128)} %param.37) | copy-start | bytes 3076
  2.2 64.7 %copy-start.24 = (bf16[2,128,128]{2,1,0:T(8,128)(2,1)S(1)}, bf16[2,128,128]{2,1,0:T(8,128)(2,1)}, u32[]{:S(2)}) copy-start(bf16[2,128,128]{2,1,0:T(8,128)(2,1)} %param.34) | copy-start | bytes 196612
  2.3 65.5 %copy-start.7 = (s32[4096]{0:T(1024)S(1)}, s32[4096]{0:T(1024)}, u32[]{:S(2)}) copy-start(s32[4096]{0:T(1024)} %param.25) | copy-start | bytes 49156
  2.9 64.9 %copy-start.8 = (s32[4096]{0:T(1024)S(1)}, s32[4096]{0:T(1024)}, u32[]{:S(2)}) copy-start(s32[4096]{0:T(1024)} %param.24) | copy-start | bytes 49156
  2.9 64.9 %copy-start.10 = (s32[1024]{0:T(1024)S(1)}, s32[1024]{0:T(1024)}, u32[]{:S(2)}) copy-start(s32[1024]{0:T(1024)} %param.28) | copy-start | bytes 12292
  2.9 71.2 %collective-permute-start = (bf16[128,128]{1,0:T(8,128)(2,1)}, bf16[128,128]{1,0:T(8,128)(2,1)}, u32[]{:S(2)}, u32[]{:S(2)}) collective-permute-start(bf16[128,128]{1,0:T(8,128)(2,1)} %get-tuple-element.408), channel_id=1, source_target_pairs={{0,32},{32,64},{64,96},{96,128},{128,160},{160,192},{192,224},{1,3... | collective-permute-start | bytes 98312 | tf_op jit(solution)/shard_map/ppermute | solution.py:21
  6.6 68.3 %collective-permute-start.1 = (bf16[128,128]{1,0:T(8,128)(2,1)}, bf16[128,128]{1,0:T(8,128)(2,1)}, u32[]{:S(2)}, u32[]{:S(2)}) collective-permute-start(bf16[128,128]{1,0:T(8,128)(2,1)} %get-tuple-element.407), channel_id=1, source_target_pairs={{32,0},{64,32},{96,64},{128,96},{160,128},{192,160},{224,192},{33,... | collective-permute-start | bytes 98312 | tf_op jit(solution)/shard_map/ppermute | solution.py:21
  8.9 66.8 %collective-permute-start.2 = (bf16[128,128]{1,0:T(8,128)(2,1)}, bf16[128,128]{1,0:T(8,128)(2,1)}, u32[]{:S(2)}, u32[]{:S(2)}) collective-permute-start(bf16[128,128]{1,0:T(8,128)(2,1)} %get-tuple-element.406), channel_id=1, source_target_pairs={{0,1},{1,2},{2,3},{3,4},{4,5},{5,6},{6,7},{7,8},{8,9},{9,10},{10,1... | collective-permute-start | bytes 98312 | tf_op jit(solution)/shard_map/ppermute | solution.py:21
  13.2 63.3 %collective-permute-start.3 = (bf16[128,128]{1,0:T(8,128)(2,1)}, bf16[128,128]{1,0:T(8,128)(2,1)S(1)}, u32[]{:S(2)}, u32[]{:S(2)}) collective-permute-start(bf16[128,128]{1,0:T(8,128)(2,1)} %get-tuple-element.405), channel_id=1, source_target_pairs={{1,0},{2,1},{3,2},{4,3},{5,4},{6,5},{7,6},{8,7},{9,8},{10,9},{11,1... | collective-permute-start | bytes 98312 | tf_op jit(solution)/shard_map/ppermute | solution.py:21
  15.7 52.1 %all-to-all-start = ((bf16[8,1,8,128]{3,2,1,0:T(8,128)(2,1)}), bf16[8,1,8,128]{3,2,1,0:T(8,128)(2,1)S(1)}, u32[]{:S(2)}, u32[]{:S(2)}) async-start(bf16[8,1,8,128]{3,2,1,0:T(8,128)(2,1)} %broadcast_in_dim.23), calls=%async_computation | async-start | bytes 32768 | tf_op jit(solution)/shard_map/all_to_all | solution.py:36
  68.8 65.3 %all-to-all-start.1 = ((bf16[32,8,8,128]{3,2,1,0:T(8,128)(2,1)}), bf16[32,8,8,128]{3,2,1,0:T(8,128)(2,1)S(1)}, u32[]{:S(2)}, u32[]{:S(2)}) async-start(bf16[32,8,8,128]{3,2,1,0:T(8,128)(2,1)} %broadcast_in_dim.24), calls=%async_computation.1 | async-start | bytes 1048576 | tf_op jit(solution)/shard_map/all_to_all | solution.py:36
  76.5 2.8 %copy-start.2 = (bf16[1536,128]{1,0:T(8,128)(2,1)}, bf16[1536,128]{1,0:T(8,128)(2,1)S(1)}, u32[]{:S(2)}) copy-start(bf16[1536,128]{1,0:T(8,128)(2,1)S(1)} %get-tuple-element.677) | copy-start | bytes 1179652 | tf_op jit(solution)/shard_map/while
  83.7 2.8 %copy-start.2 = (bf16[1536,128]{1,0:T(8,128)(2,1)}, bf16[1536,128]{1,0:T(8,128)(2,1)S(1)}, u32[]{:S(2)}) copy-start(bf16[1536,128]{1,0:T(8,128)(2,1)S(1)} %get-tuple-element.677) | copy-start | bytes 1179652 | tf_op jit(solution)/shard_map/while
  98.0 2.8 %copy-start.2 = (bf16[1536,128]{1,0:T(8,128)(2,1)}, bf16[1536,128]{1,0:T(8,128)(2,1)S(1)}, u32[]{:S(2)}) copy-start(bf16[1536,128]{1,0:T(8,128)(2,1)S(1)} %get-tuple-element.677) | copy-start | bytes 1179652 | tf_op jit(solution)/shard_map/while
  112.4 2.8 %copy-start.2 = (bf16[1536,128]{1,0:T(8,128)(2,1)}, bf16[1536,128]{1,0:T(8,128)(2,1)S(1)}, u32[]{:S(2)}) copy-start(bf16[1536,128]{1,0:T(8,128)(2,1)S(1)} %get-tuple-element.677) | copy-start | bytes 1179652 | tf_op jit(solution)/shard_map/while
  137.0 3.5 %copy-start.25 = (bf16[2,128,128]{2,1,0:T(8,128)(2,1)S(1)}, bf16[2,128,128]{2,1,0:T(8,128)(2,1)}, u32[]{:S(2)}) copy-start(bf16[2,128,128]{2,1,0:T(8,128)(2,1)} %param.34) | copy-start | bytes 196612
  137.1 3.5 %copy-start.29 = (f32[128]{0:T(128)S(1)}, f32[128]{0:T(128)}, u32[]{:S(2)}) copy-start(f32[128]{0:T(128)} %copy-done.28) | copy-start | bytes 1540
  137.2 4.2 %copy-start.9 = (f32[1,3,128]{2,0,1:T(1,128)S(1)}, f32[1,3,128]{2,0,1:T(1,128)}, u32[]{:S(2)}) copy-start(f32[1,3,128]{2,0,1:T(1,128)} %get-tuple-element.415) | copy-start | bytes 4612
  138.2 17.9 %copy-start.6 = (f32[1,128]{1,0:T(1,128)S(1)}, f32[1,128]{1,0:T(1,128)}, u32[]{:S(2)}) copy-start(f32[1,128]{1,0:T(1,128)} %get-tuple-element.696) | copy-start | bytes 1540
  138.3 12.4 %collective-permute-start.4 = (bf16[128,128]{0,1:T(8,128)(2,1)S(1)}, bf16[128,128]{0,1:T(8,128)(2,1)S(1)}, u32[]{:S(2)}, u32[]{:S(2)}) collective-permute-start(bf16[128,128]{0,1:T(8,128)(2,1)S(1)} %get-tuple-element.404), channel_id=1, source_target_pairs={{0,32},{32,64},{64,96},{96,128},{128,160},{160,192},{192,224},{1,3... | collective-permute-start | bytes 98312 | tf_op jit(solution)/shard_map/ppermute | solution.py:21
  141.6 9.1 %collective-permute-start.5 = (bf16[128,128]{0,1:T(8,128)(2,1)S(1)}, bf16[128,128]{0,1:T(8,128)(2,1)S(1)}, u32[]{:S(2)}, u32[]{:S(2)}) collective-permute-start(bf16[128,128]{0,1:T(8,128)(2,1)S(1)} %get-tuple-element.403), channel_id=1, source_target_pairs={{32,0},{64,32},{96,64},{128,96},{160,128},{192,160},{224,192},{33,... | collective-permute-start | bytes 98312 | tf_op jit(solution)/shard_map/ppermute | solution.py:21
  144.6 6.1 %collective-permute-start.6 = (bf16[128,128]{0,1:T(8,128)(2,1)S(1)}, bf16[128,128]{0,1:T(8,128)(2,1)S(1)}, u32[]{:S(2)}, u32[]{:S(2)}) collective-permute-start(bf16[128,128]{0,1:T(8,128)(2,1)S(1)} %get-tuple-element.402), channel_id=1, source_target_pairs={{0,1},{1,2},{2,3},{3,4},{4,5},{5,6},{6,7},{7,8},{8,9},{9,10},{10,1... | collective-permute-start | bytes 98312 | tf_op jit(solution)/shard_map/ppermute | solution.py:21
  148.5 7.3 %collective-permute-start.7 = (bf16[128,128]{0,1:T(8,128)(2,1)S(1)}, bf16[128,128]{0,1:T(8,128)(2,1)S(1)}, u32[]{:S(2)}, u32[]{:S(2)}) collective-permute-start(bf16[128,128]{0,1:T(8,128)(2,1)S(1)} %get-tuple-element.401), channel_id=1, source_target_pairs={{1,0},{2,1},{3,2},{4,3},{5,4},{6,5},{7,6},{8,7},{9,8},{10,9},{11,1... | collective-permute-start | bytes 98312 | tf_op jit(solution)/shard_map/ppermute | solution.py:21
  156.1 48.9 %copy-start.20 = (f32[128]{0:T(128)S(1)}, f32[128]{0:T(128)}, u32[]{:S(2)}) copy-start(f32[128]{0:T(128)} %get-tuple-element.414) | copy-start | bytes 1540
  156.1 48.9 %copy-start.23 = (bf16[2,384,128]{2,1,0:T(8,128)(2,1)S(1)}, bf16[2,384,128]{2,1,0:T(8,128)(2,1)}, u32[]{:S(2)}) copy-start(bf16[2,384,128]{2,1,0:T(8,128)(2,1)} %param.33) | copy-start | bytes 589828
  (30 other events, 46.8 us)
where the time goes:
time: 209 us; the launch traced here: 208 us
  matrix products  88.1 us (42%)
  blocking collectives  38.7 us (19%)
  starting transfers between devices  37.5 us (18%)
  local copies, waits for them, and re-layouts  27.1 us (13%)
  other arithmetic  8.48 us (4%)
  waiting for transfers between devices  5.17 us (2%)
    psum x4, blocking collectives, one_axis_at_a_time(): return functools.reduce(lax.psum, axes, value)  38.7 us
    dot_general x20, matrix products, lookup(): jnp.dot(picker, table, preferred_element_type=jnp.float32)  28 us
    dot_general x18, matrix products, norm_tail(): y_val = jnp.dot(hidden, w_out, preferred_element_type=jnp.float32) + b_out  25.6 us
    ppermute x8, starting transfers between devices, passed_along(): return lax.ppermute(value, axis, pairs)  23.5 us
    dot_general x16, matrix products, one_block(): jnp.dot(recv_hot, nodes, preferred_element_type=jnp.float32)  20.7 us
    all_to_all x2, starting transfers between devices, from_everyone(): return lax.all_to_all(copies, axis, split_axis=0, concat_axis=0, tiled=True)  14 us
    dot_general x16, matrix products, one_block(): lax.dot_general(recv_hot, fresh, (((0,), (0,)), ((), ())), preferred_elem...  12.3 us
    dynamic_slice x32, local copies, waits for them, and re-layouts, edge_and_sum(): summed, fresh = lax.scan(one_block, start, items)  8.36 us
  transfers between devices with their start and end apart: 10, of which 1 were waited for; matrix products, arithmetic and copies ran while one was open for 31% of the time, Pallas kernels for 0%

commit v1 on v0

v1 whole, which is shorter than its diff:
```python
import functools
import math

import jax
import jax.numpy as jnp
from jax import lax
from jax.experimental import pallas as pl
from jax.experimental.pallas import tpu as pltpu
from jax.sharding import Mesh
from jax.sharding import PartitionSpec as P

LAYERS = 2
COL = ("col_0", "col_1", "col_2")
ROW_COL = ("row", "col_0", "col_1", "col_2")
EPS = 1e-05
W = 128
TILE = 512
BF = jnp.bfloat16
F32 = jnp.float32
VM = pltpu.VMEM


def dot(a, b):
    return jnp.dot(a, b, preferred_element_type=F32)


def columns(stack, count):
    turned = jnp.transpose(stack)
    return [
        jnp.broadcast_to(turned[:, k : k + 1], (W, W)).astype(jnp.int16) for k in range(count)
    ]


def column_hot(col, count):
    lane = lax.broadcasted_iota(jnp.int16, (1, W), 1)
    one, zero = jnp.ones((), BF), jnp.zeros((), BF)
    pieces = [
        jnp.where(col == lane + jnp.int16(W * c), one, zero) for c in range(count // W)
    ]
    return jnp.concatenate(pieces, axis=1)


def row_hot(row, count):
    spread = jnp.broadcast_to(row, (16, W)).astype(jnp.int16)
    at = lax.broadcasted_iota(jnp.int16, (16, W), 0)
    one, zero = jnp.ones((), BF), jnp.zeros((), BF)
    pieces = [jnp.where(spread == at + jnp.int16(16 * c), one, zero) for c in range(count // 16)]
    return jnp.concatenate(pieces, axis=0)


def split2(value):
    high = value.astype(BF)
    low = (value - high.astype(F32)).astype(BF)
    return high, low


def split3(value):
    high = value.astype(BF)
    rest = value - high.astype(F32)
    mid = rest.astype(BF)
    low = (rest - mid.astype(F32)).astype(BF)
    return high, mid, low


def centred_weights(w_out, b_out):
    full = w_out.astype(F32)
    full = full - jnp.mean(full, axis=1, keepdims=True)
    high, low = split2(full)
    return jnp.concatenate([high, low], axis=1), b_out - jnp.mean(b_out, axis=1, keepdims=True)


def norm_tail(pre, w_two, b_centred, gain, shift):
    hidden = jnp.maximum(pre, 0.0).astype(BF)
    both = dot(hidden, w_two)
    centred = both[:, :W] + both[:, W:] + b_centred
    averager = jnp.full((W, W), 1.0 / W, BF)
    spread = dot((centred * centred).astype(BF), averager)
    return centred * lax.rsqrt(spread + EPS) * gain + shift


def picked_rows(table_two, half_rows, stack, count):
    cols = columns(stack, count)
    col = jnp.concatenate(cols, axis=0)
    hot = column_hot(col & jnp.int16(half_rows - 1), half_rows)
    both = dot(hot, table_two)
    upper = col.astype(jnp.int32) >= half_rows
    return jnp.where(upper, both[:, W:], both[:, :W]).astype(BF)


def phases(first, second, odd):
    return jnp.where(odd, second, first), jnp.where(odd, first, second)


def send_rows(table_two, half_rows, send_ref):
    row_odd = lax.rem(lax.axis_index("row"), 2) == 1
    col_odd = lax.axis_index("col_2") == 1
    index = [send_ref[0, k : k + 1, :] for k in range(4)]
    index_a, index_b = phases(index[0], index[1], row_odd)
    index_c, index_d = phases(index[2], index[3], col_odd)
    stack = jnp.concatenate([index_a, index_b, index_c, index_d] + [index_a] * 4, axis=0)
    return picked_rows(table_two, half_rows, stack, 4)


def start_kernel(nodes_ref, send_ref, context_ref, payload_ref, *picked_refs):
    nodes = nodes_ref[...]
    half = nodes.shape[0] // 2
    two = jnp.concatenate([nodes[:half], nodes[half:]], axis=1)
    picked = send_rows(two, half, send_ref)
    for k, ref in enumerate(picked_refs):
        ref[...] = picked[W * k : W * (k + 1)]
    local_sum = jnp.sum(nodes.astype(F32), axis=0, keepdims=True)
    high, mid, low = split3(local_sum)
    block = jnp.concatenate(
        [
            context_ref[...].astype(F32),
            high.astype(F32),
            mid.astype(F32),
            low.astype(F32),
            jnp.zeros((5, W), F32),
        ],
        axis=0,
    ).astype(BF)
    for k in range(payload_ref.shape[0]):
        payload_ref[k] = block


def middle_kernel(got_ref, payload_ref):
    got = [got_ref[k].astype(F32) for k in range(got_ref.shape[0])]
    total = functools.reduce(
        lambda a, b: a + b, [g[8:9] + (g[9:10] + g[10:11]) for g in got]
    )
    high, mid, low = split3(total)
    block = jnp.concatenate(
        [g[:8] for g in got]
        + [high.astype(F32), mid.astype(F32), low.astype(F32), jnp.zeros((13, W), F32)],
        axis=0,
    ).astype(BF)
    for k in range(payload_ref.shape[0]):
        payload_ref[k] = block


def edge_kernel(
    layer,
    nodes_ref,
    halo_a,
    halo_b,
    halo_c,
    halo_d,
    senders_ref,
    receivers_ref,
    edges_ref,
    w_in_ref,
    w_out_ref,
    bias_ref,
    gain_ref,
    fresh_ref,
    summed_ref,
    send_table,
    recv_table,
    send_col,
    recv_col,
    acc,
    w_two,
):
    step = pl.program_id(0)
    node_count = nodes_ref.shape[0]
    extent = node_count + 4 * W
    send_half = extent // 2
    recv_half = node_count // 2

    @pl.when(step == 0)
    def _():
        nodes = nodes_ref[...]
        ext = jnp.concatenate(
            [nodes, halo_a[...], halo_b[...], halo_c[...], halo_d[...]], axis=0
        )
        from_send = dot(ext, w_in_ref[0, :W]).astype(BF)
        from_recv = dot(nodes, w_in_ref[0, W : 2 * W]).astype(BF)
        send_table[:send_half, :W] = from_send[:send_half]
        send_table[:send_half, W:] = from_send[send_half:]
        send_table[send_half:, :W] = w_in_ref[0, 2 * W :]
        send_table[send_half:, W:] = w_in_ref[0, 2 * W :]
        recv_table[:, :W] = from_recv[:recv_half]
        recv_table[:, W:] = from_recv[recv_half:]
        w_two[...] = centred_weights(w_out_ref[0], bias_ref[0, 1:2])[0]
        senders = senders_ref[...]
        row_flip = jnp.where(lax.rem(lax.axis_index("row"), 2) == 1, 0, W)
        col_flip = jnp.where(lax.axis_index("col_2") == 1, 0, W)
        flip = jnp.where(senders < node_count + 2 * W, row_flip, col_flip)
        senders = jnp.where(senders < node_count, senders, senders ^ flip)
        receivers = receivers_ref[...]
        for values, ref in ((senders, send_col), (receivers, recv_col)):
            count = values.shape[0]
            for k, block in enumerate(columns(values, count)):
                ref[W * k : W * (k + 1)] = block
        acc[...] = jnp.zeros_like(acc)

    at = pl.ds(pl.multiple_of(step * TILE, TILE), TILE)
    edges = edges_ref[...]
    send16 = send_col[at]
    recv16 = recv_col[at]
    send_local = jnp.where(send16 >= jnp.int16(send_half), send16 - jnp.int16(send_half), send16)
    send_hot = column_hot(send_local, send_half)
    recv_hot = column_hot(recv16 & jnp.int16(recv_half - 1), recv_half)
    both_s = dot(jnp.concatenate([send_hot, edges], axis=1), send_table[...])
    both_r = dot(recv_hot, recv_table[...])
    upper_s = send16.astype(jnp.int32) >= send_half
    upper_r = recv16.astype(jnp.int32) >= recv_half
    pre = (
        jnp.where(upper_s, both_s[:, W:], both_s[:, :W])
        + jnp.where(upper_r, both_r[:, W:], both_r[:, :W])
        + bias_ref[0, 0:1]
    )
    b_out = bias_ref[0, 1:2]
    b_centred = b_out - jnp.mean(b_out, axis=1, keepdims=True)
    tail = norm_tail(
        pre, w_two[...], b_centred, gain_ref[layer : layer + 1], bias_ref[0, 2:3]
    )
    fresh = (edges.astype(F32) + tail).astype(BF)
    fresh_ref[...] = fresh
    lower16 = recv16 < jnp.int16(recv_half)
    zero = jnp.zeros((), BF)
    fresh_two = jnp.concatenate(
        [jnp.where(lower16, fresh, zero), jnp.where(lower16, zero, fresh)], axis=1
    )
    per = TILE // W
    rows = receivers_ref[pl.ds(step * per, per)] & (recv_half - 1)
    turned = jnp.concatenate(
        [row_hot(rows[k : k + 1], recv_half) for k in range(per)], axis=1
    )
    acc[...] += dot(turned, fresh_two)

    @pl.when(step == pl.num_programs(0) - 1)
    def _():
        summed_ref[:recv_half] = acc[:, :W].astype(BF)
        summed_ref[recv_half:] = acc[:, W:].astype(BF)


def whole(shape):
    return pl.BlockSpec(shape, lambda i: (0,) * len(shape))


def of_layer(shape, layer):
    return pl.BlockSpec((1, *shape[1:]), lambda i: (layer,) + (0,) * (len(shape) - 1))


def edge_step(layer, nodes, halo, senders, receivers, edges, w_in, w_out, bias, gain):
    node_count, edge_count = nodes.shape[0], edges.shape[0]
    half, ext_half = node_count // 2, (node_count + 4 * W) // 2
    steps = edge_count // TILE
    flops = 2 * edge_count * W * (2 * ext_half + 4 * half + 8 * W)
    return pl.pallas_call(
        functools.partial(edge_kernel, layer),
        grid=(steps,),
        in_specs=[
            whole(nodes.shape),
            *[whole((W, W))] * 4,
            whole(senders.shape),
            whole(receivers.shape),
            pl.BlockSpec((TILE, W), lambda i: (i, 0)),
            of_layer(w_in.shape, layer),
            of_layer(w_out.shape, layer),
            of_layer(bias.shape, layer),
            whole(gain.shape),
        ],
        out_specs=[pl.BlockSpec((TILE, W), lambda i: (i, 0)), whole(nodes.shape)],
        out_shape=[
            jax.ShapeDtypeStruct(edges.shape, BF),
            jax.ShapeDtypeStruct(nodes.shape, BF),
        ],
        scratch_shapes=[
            VM((ext_half + W, 2 * W), BF),
            VM((half, 2 * W), BF),
            VM((edge_count, W), jnp.int16),
            VM((edge_count, W), jnp.int16),
            VM((half, 2 * W), F32),
            VM((W, 2 * W), BF),
        ],
        compiler_params=pltpu.CompilerParams(dimension_semantics=("arbitrary",)),
        cost_estimate=pl.CostEstimate(
            flops=flops, bytes_accessed=4 * edge_count * W, transcendentals=0
        ),
        name=f"edges_{layer}",
    )(nodes, *halo, senders, receivers, edges, w_in, w_out, bias, gain)


def node_update(layer, nodes, summed, context, pooled, w_in_ref, wg_ref, w_out_ref, bias_ref, gain_ref):
    parts = jnp.concatenate(
        [p.astype(F32) for p in split3(pooled)] + [jnp.zeros((13, W), F32)], axis=0
    ).astype(BF)
    through = dot(parts, wg_ref[0])
    shift_in = bias_ref[0, 0:1] + (through[0:1] + (through[1:2] + through[2:3]))
    w_two, b_centred = centred_weights(w_out_ref[0], bias_ref[0, 1:2])
    feats = jnp.concatenate([nodes, summed, context], axis=1)
    pre = dot(feats, w_in_ref[0]) + shift_in
    tail = norm_tail(pre, w_two, b_centred, gain_ref[layer : layer + 1], bias_ref[0, 2:3])
    return (nodes.astype(F32) + tail).astype(BF)


def first_node_kernel(
    nodes_ref,
    summed_ref,
    table_ref,
    region_ref,
    send_ref,
    w_in_ref,
    wg_ref,
    w_out_ref,
    bias_ref,
    gain_ref,
    nodes_out,
    context_out,
    pooled_out,
    a_out,
    b_out,
    c_out,
    d_out,
    table_two,
    fresh_two,
):
    groups, _, _ = table_ref.shape
    own = 8 * 8
    half_groups = groups // 2
    half = half_groups * own
    total = jnp.zeros((1, W), F32)
    for g in range(groups):
        top = own * (g % half_groups)
        side = W * (g // half_groups)
        table_two[top : top + own, side : side + W] = table_ref[g, :own]
        tail = table_ref[g, own : own + 16].astype(F32)
        total = total + (tail[0:1] + (tail[1:2] + tail[2:3]))
    node_count = nodes_ref.shape[0]
    everyone = node_count * 8 * groups
    pooled = total / math.sqrt(everyone)
    pooled_out[...] = pooled
    region = region_ref[...]
    place = ((region >> 3) & (groups - 1)) * own + (region >> 8) * 8 + (region & 7)
    node_half = node_count // 2
    context = picked_rows(table_two[...], half, place, place.shape[0])
    context_out[...] = context
    for k in range(4):
        rows = slice(k * 256, (k + 1) * 256)
        fresh = node_update(
            0,
            nodes_ref[rows],
            summed_ref[rows],
            context[rows],
            pooled,
            w_in_ref,
            wg_ref,
            w_out_ref,
            bias_ref,
            gain_ref,
        )
        nodes_out[rows] = fresh
        top = (k * 256) % node_half
        side = W * ((k * 256) // node_half)
        fresh_two[top : top + 256, side : side + W] = fresh
    picked = send_rows(fresh_two[...], node_half, send_ref)
    for k, ref in enumerate((a_out, b_out, c_out, d_out)):
        ref[...] = picked[W * k : W * (k + 1)]


def last_node_kernel(
    layer,
    nodes_ref,
    summed_ref,
    context_ref,
    pooled_ref,
    w_in_ref,
    wg_ref,
    w_out_ref,
    bias_ref,
    gain_ref,
    nodes_out,
):
    nodes_out[...] = node_update(
        layer,
        nodes_ref[...],
        summed_ref[...],
        context_ref[...],
        pooled_ref[...],
        w_in_ref,
        wg_ref,
        w_out_ref,
        bias_ref,
        gain_ref,
    )


def exchanged(block, axis, phase):
    devices = lax.axis_size(axis)
    pairs = []
    for i in range(phase, devices - 1, 2):
        pairs += [(i, i + 1), (i + 1, i)]
    return lax.ppermute(block, axis, pairs)


def halo_of(picked):
    return [
        exchanged(picked[0], "row", 0),
        exchanged(picked[1], "row", 1),
        exchanged(picked[2], COL, 0),
        exchanged(picked[3], COL, 1),
    ]


def to_everyone(copies, axis):
    return lax.all_to_all(copies, axis, split_axis=0, concat_axis=0, tiled=True)


def local(
    node_latent,
    edge_latent,
    senders,
    receivers,
    send_index,
    context_table,
    region,
    edge_w1,
    edge_w2,
    edge_bias,
    edge_gain,
    node_w1,
    node_wg,
    node_w2,
    node_bias,
    node_gain,
):
    n_row, n_col = lax.axis_size("row"), lax.axis_size(COL)
    block = jax.ShapeDtypeStruct((W, W), BF)
    payload, *picked = pl.pallas_call(
        start_kernel,
        out_shape=[jax.ShapeDtypeStruct((n_row, 16, W), BF)] + [block] * 4,
        name="start",
    )(node_latent, send_index, context_table)
    halo = halo_of(picked)
    by_row = to_everyone(payload, "row")
    second = pl.pallas_call(
        middle_kernel,
        out_shape=jax.ShapeDtypeStruct((n_col, 80, W), BF),
        name="middle",
    )(by_row)
    table = to_everyone(second, COL)
    senders = senders.reshape(-1, W)
    receivers = receivers.reshape(-1, W)
    edges, summed = edge_step(
        0, node_latent, halo, senders, receivers, edge_latent, edge_w1, edge_w2, edge_bias, edge_gain
    )
    node_specs = [
        of_layer(node_w1.shape, 0),
        of_layer(node_wg.shape, 0),
        of_layer(node_w2.shape, 0),
        of_layer(node_bias.shape, 0),
        whole(node_gain.shape),
    ]
    node_count = node_latent.shape[0]
    region = region.reshape(-1, W)
    nodes, context, pooled, *picked = pl.pallas_call(
        first_node_kernel,
        grid=(1,),
        in_specs=[
            whole(node_latent.shape),
            whole(node_latent.shape),
            whole(table.shape),
            whole(region.shape),
            whole(send_index.shape),
            *node_specs,
        ],
        out_specs=[whole(node_latent.shape)] * 2 + [whole((1, W))] + [whole((W, W))] * 4,
        out_shape=[jax.ShapeDtypeStruct(node_latent.shape, BF)] * 2
        + [jax.ShapeDtypeStruct((1, W), F32)]
        + [block] * 4,
        scratch_shapes=[
            VM((n_col // 2 * 64, 2 * W), BF),
            VM((node_count // 2, 2 * W), BF),
        ],
        name="nodes_0",
    )(node_latent, summed, table, region, send_index, node_w1, node_wg, node_w2, node_bias, node_gain)
    halo = halo_of(picked)
    edges, summed = edge_step(
        1, nodes, halo, senders, receivers, edges, edge_w1, edge_w2, edge_bias, edge_gain
    )
    rows = 256
    strip = pl.BlockSpec((rows, W), lambda i: (i, 0))
    nodes = pl.pallas_call(
        functools.partial(last_node_kernel, 1),
        grid=(node_count // rows,),
        in_specs=[
            strip,
            strip,
            strip,
            whole((1, W)),
            of_layer(node_w1.shape, 1),
            of_layer(node_wg.shape, 1),
            of_layer(node_w2.shape, 1),
            of_layer(node_bias.shape, 1),
            whole(node_gain.shape),
        ],
        out_specs=strip,
        out_shape=jax.ShapeDtypeStruct(nodes.shape, BF),
        name="nodes_1",
    )(nodes, summed, context, pooled, node_w1, node_wg, node_w2, node_bias, node_gain)
    return (nodes, edges)


def solution(mesh):
    finer = Mesh(
        mesh.devices.reshape(mesh.shape["row"], 4, 4, 2), ("row", "col_0", "col_1", "col_2")
    )
    placed = (
        P(ROW_COL, None),
        P(ROW_COL, None),
        P(ROW_COL),
        P(ROW_COL),
        P(ROW_COL, None, None),
        P(ROW_COL, None),
        P(ROW_COL),
        P(),
        P(),
        P(),
        P(),
        P(),
        P(),
        P(),
        P(),
        P(),
    )
    return jax.shard_map(
        local,
        mesh=finer,
        in_specs=placed,
        out_specs=(P(ROW_COL, None), P(ROW_COL, None)),
        check_vma=False,
    )
```

time: 209 us -> 92.5 us (0.44)
  matrix products: 88.1 us -> 0 us
  Pallas kernels: 0 us -> 43.1 us
  blocking collectives: 38.7 us -> 13.8 us
  local copies, waits for them, and re-layouts: 27.1 us -> 3.22 us
  starting transfers between devices: 37.5 us -> 23.3 us
  other arithmetic: 8.48 us -> 0 us
  waiting for transfers between devices: 5.17 us -> 7.57 us
    dot_general x72 -> x0, matrix products: 88.1 us -> none  [the longest x20 28 us: lookup(): jnp.dot(picker, table, preferred_element_type=jnp.float32)]
    pallas_call x0 -> x6, Pallas kernels: none -> 43.1 us  [the longest x2 30 us: edge_step(): pl.pallas_call(functools.partial(edge_kernel, layer), grid=(steps,), in_s...]
    psum x4 -> x0, blocking collectives: 38.7 us -> none  [one_axis_at_a_time(): return functools.reduce(lax.psum, axes, value)]
    all_to_all x0 -> x1, blocking collectives: none -> 13.8 us  [to_everyone(): return lax.all_to_all(copies, axis, split_axis=0, concat_axis=0, tiled=True)]
    ppermute x8, starting transfers between devices: 23.5 us -> 13.8 us  [exchanged(): return lax.ppermute(block, axis, pairs)]
    dynamic_slice x34 -> x0, local copies, waits for them, and re-layouts: 8.38 us -> none  [the longest x32 8.36 us: edge_and_sum(): summed, fresh = lax.scan(one_block, start, items)]
    dynamic_update_slice x16 -> x0, local copies, waits for them, and re-layouts: 6.31 us -> none  [edge_and_sum(): summed, fresh = lax.scan(one_block, start, items)]
    dynamic_update_slice x8 -> x0, other arithmetic: 5.79 us -> none  [edge_and_sum(): summed, fresh = lax.scan(one_block, start, items)]
  transfers between devices with their start and end apart: 10 -> 9, of which waited for: 1 -> 2; matrix products, arithmetic and copies ran while one was open for 31% -> 1% of each run, Pallas kernels for 0% -> 16%
where the time goes in v1:
time: 92.5 us; the launch traced here: 91.8 us
  Pallas kernels  43.1 us (47%)
  starting transfers between devices  23.3 us (25%)
  blocking collectives  13.8 us (15%)
  waiting for transfers between devices  7.57 us (8%)
  local copies, waits for them, and re-layouts  3.22 us (3%)
    pallas_call x2, Pallas kernels, edge_step(): pl.pallas_call(functools.partial(edge_kernel, layer), grid=(steps,), in_s...  30 us
    ppermute x8, starting transfers between devices, exchanged(): return lax.ppermute(block, axis, pairs)  13.8 us
    all_to_all x1, blocking collectives, to_everyone(): return lax.all_to_all(copies, axis, split_axis=0, concat_axis=0, tiled=True)  13.8 us
    all_to_all x1, starting transfers between devices, to_everyone(): return lax.all_to_all(copies, axis, split_axis=0, concat_axis=0, tiled=True)  9.42 us
    ppermute x8, waiting for transfers between devices, exchanged(): return lax.ppermute(block, axis, pairs)  7.57 us
    pallas_call x1, Pallas kernels, local(): pl.pallas_call(first_node_kernel, grid=(1,), in_specs=[whole(node_latent....  5.16 us
    pallas_call x1, Pallas kernels, local(): pl.pallas_call(functools.partial(last_node_kernel, 1), grid=(node_count /...  4.16 us
    unnamed x32, local copies, waits for them, and re-layouts  3.22 us
  transfers between devices with their start and end apart: 9, of which 2 were waited for; matrix products, arithmetic and copies ran while one was open for 1% of the time, Pallas kernels for 16%

profile of v1, /device:TPU:39, one launch (start us, length us, event | category | flops | bytes accessed | tf_op | source)
XLA Modules:
  0.0 91.8 jit_solution(15004877362327250066)
XLA Ops:
  0.6 2.1 %start.1 = (bf16[8,16,128]{2,1,0:T(8,128)(2,1)}, bf16[128,128]{1,0:T(8,128)(2,1)}, bf16[128,128]{1,0:T(8,128)(2,1)}, bf16[128,128]{1,0:T(8,128)(2,1)}, bf16[128,128]{1,0:T(8,128)(2,1)}) custom-call(bf16[1024,128]{1,0:T(8,128)(2,1)} %nodes_ref.5, s32[1,4,128]{2,1,0:T(4,128)} %send_ref.3, bf16[8,128]{1,0:T(8,128)(2,1)} %context_ref.1), custom_call_target="tpu_custom_call" | custom-call | tf_op jit(solution)/shard_map/start/pallas_call | solution.py:432
  2.7 13.8 %all_to_all.10.got_ref = bf16[8,16,128]{2,1,0:T(8,128)(2,1)} all-to-all(bf16[8,16,128]{2,1,0:T(8,128)(2,1)} %get-tuple-element.23), channel_id=1, replica_groups=mesh['row'=8,'col_0'=4,'col_1'=4,'col_2'=2] {'row'}, dimensions={0} | all-to-all | bytes 65536 | tf_op jit(solution)/shard_map/all_to_all | solution.py:409
  16.5 1.7 %middle.1 = bf16[32,80,128]{2,1,0:T(8,128)(2,1)} custom-call(bf16[8,16,128]{2,1,0:T(8,128)(2,1)} %all_to_all.10.got_ref), custom_call_target="tpu_custom_call" | custom-call | tf_op jit(solution)/shard_map/middle/pallas_call | solution.py:439
  18.2 9.4 %all-to-all-start.1 = ((bf16[32,80,128]{2,1,0:T(8,128)(2,1)}), bf16[32,80,128]{2,1,0:T(8,128)(2,1)S(1)}, u32[]{:S(2)}, u32[]{:S(2)}) async-start(bf16[32,80,128]{2,1,0:T(8,128)(2,1)} %middle.1), calls=%async_computation.1 | async-start | bytes 1310720 | tf_op jit(solution)/shard_map/all_to_all | solution.py:409
  27.6 0.0 copy-start.1
  27.6 1.3 %collective-permute-start = (bf16[128,128]{1,0:T(8,128)(2,1)S(1)}, bf16[128,128]{1,0:T(8,128)(2,1)S(1)}, u32[]{:S(2)}, u32[]{:S(2)}) collective-permute-start(bf16[128,128]{1,0:T(8,128)(2,1)S(1)} %copy-done.8), channel_id=1, source_target_pairs={{0,32},{32,0},{64,96},{96,64},{128,160},{160,128},{192,224},{224,1... | collective-permute-start | bytes 98312 | tf_op jit(solution)/shard_map/ppermute | solution.py:396
  28.9 1.9 %collective-permute-start.1 = (bf16[128,128]{1,0:T(8,128)(2,1)S(1)}, bf16[128,128]{1,0:T(8,128)(2,1)S(1)}, u32[]{:S(2)}, u32[]{:S(2)}) collective-permute-start(bf16[128,128]{1,0:T(8,128)(2,1)S(1)} %copy-done.5), channel_id=1, source_target_pairs={{32,64},{64,32},{96,128},{128,96},{160,192},{192,160},{33,65},{65,... | collective-permute-start | bytes 98312 | tf_op jit(solution)/shard_map/ppermute | solution.py:396
  30.8 0.8 collective-permute-start.2
  31.6 3.0 %collective-permute-start.3 = (bf16[128,128]{1,0:T(8,128)(2,1)S(1)}, bf16[128,128]{1,0:T(8,128)(2,1)S(1)}, u32[]{:S(2)}, u32[]{:S(2)}) collective-permute-start(bf16[128,128]{1,0:T(8,128)(2,1)S(1)} %copy-done.3), channel_id=1, source_target_pairs={{1,2},{2,1},{3,4},{4,3},{5,6},{6,5},{7,8},{8,7},{9,10},{10,9},{11,... | collective-permute-start | bytes 98312 | tf_op jit(solution)/shard_map/ppermute | solution.py:396
  34.6 0.6 copy.18.bias_ref
  35.2 0.6 copy.19.bias_ref
  35.8 0.0 collective-permute-done.1.halo_b
  35.8 0.0 collective-permute-done.2.halo_c
  35.8 3.2 %collective-permute-done.3.halo_d = bf16[128,128]{1,0:T(8,128)(2,1)S(1)} collective-permute-done((bf16[128,128]{1,0:T(8,128)(2,1)S(1)}, bf16[128,128]{1,0:T(8,128)(2,1)S(1)}, u32[]{:S(2)}, u32[]{:S(2)}) %collective-permute-start.3) | collective-permute-done | bytes 32800 | tf_op jit(solution)/shard_map/ppermute | solution.py:396
  39.1 0.6 copy-done.14
  39.7 15.0 %edges_0.1 = (bf16[4096,128]{1,0:T(8,128)(2,1)}, bf16[1024,128]{1,0:T(8,128)(2,1)}) custom-call(bf16[1024,128]{1,0:T(8,128)(2,1)} %nodes_ref.5, bf16[128,128]{1,0:T(8,128)(2,1)} %copy-done.6, bf16[128,128]{1,0:T(8,128)(2,1)} %copy-done.9, bf16[128,128]{1,0:T(8,128)(2,1)} %copy-done.11, bf16[128,128]{1,0:T(8,128)(2,1)} %copy-done.14, s32[32,128]{1,0:T(8,128)} %bitcast.4, ...), custom_call_target="tpu_custom_call" | custom-call | flops 4831838208 | bytes 2097152 | tf_op jit(solution)/shard_map/edges_0/pallas_call | solution.py:252
  54.7 0.0 all-to-all-done.1.table_ref
  54.7 0.0 copy-start
  54.7 0.8 copy-done
  55.5 5.2 %nodes_0.1 = (bf16[1024,128]{1,0:T(8,128)(2,1)}, bf16[1024,128]{1,0:T(8,128)(2,1)}, f32[1,128]{1,0:T(1,128)}, bf16[128,128]{1,0:T(8,128)(2,1)}, bf16[128,128]{1,...) custom-call(bf16[1024,128]{1,0:T(8,128)(2,1)} %nodes_ref.5, ...), custom_call_target="tpu_custom_call" | custom-call | tf_op jit(solution)/shard_map/nodes_0/pallas_call | solution.py:459
  60.7 0.2 collective-permute-start.4
  60.9 3.4 %collective-permute-start.5 = (bf16[128,128]{1,0:T(8,128)(2,1)}, bf16[128,128]{1,0:T(8,128)(2,1)S(1)}, u32[]{:S(2)}, u32[]{:S(2)}) collective-permute-start(bf16[128,128]{1,0:T(8,128)(2,1)} %get-tuple-element.26), channel_id=1, source_target_pairs={{32,64},{64,32},{96,128},{128,96},{160,192},{192,160},{33,65},{65,... | collective-permute-start | bytes 98312 | tf_op jit(solution)/shard_map/ppermute | solution.py:396
  64.3 0.1 collective-permute-start.6
  64.4 3.2 %collective-permute-start.7 = (bf16[128,128]{1,0:T(8,128)(2,1)}, bf16[128,128]{1,0:T(8,128)(2,1)S(1)}, u32[]{:S(2)}, u32[]{:S(2)}) collective-permute-start(bf16[128,128]{1,0:T(8,128)(2,1)} %get-tuple-element.28), channel_id=1, source_target_pairs={{1,2},{2,1},{3,4},{4,3},{5,6},{6,5},{7,8},{8,7},{9,10},{10,9},{11,... | collective-permute-start | bytes 98312 | tf_op jit(solution)/shard_map/ppermute | solution.py:396
  67.6 0.0 collective-permute-done.4.halo_a
  67.6 0.0 copy-start.7
  67.6 0.0 collective-permute-done.5.halo_b
  67.6 0.0 collective-permute-done.6.halo_c
  67.6 4.3 %collective-permute-done.7.halo_d = bf16[128,128]{1,0:T(8,128)(2,1)S(1)} collective-permute-done((bf16[128,128]{1,0:T(8,128)(2,1)}, bf16[128,128]{1,0:T(8,128)(2,1)S(1)}, u32[]{:S(2)}, u32[]{:S(2)}) %collective-permute-start.7) | collective-permute-done | bytes 32800 | tf_op jit(solution)/shard_map/ppermute | solution.py:396
  72.0 0.6 copy-done.13
  72.6 15.0 %edges_1.1 = (bf16[4096,128]{1,0:T(8,128)(2,1)}, bf16[1024,128]{1,0:T(8,128)(2,1)}) custom-call(bf16[1024,128]{1,0:T(8,128)(2,1)} %get-tuple-element.24.nodes_ref, bf16[128,128]{1,0:T(8,128)(2,1)} %copy-done.7, bf16[128,128]{1,0:T(8,128)(2,1)} %copy-done.10, bf16[128,128]{1,0:T(8,128)(2,1)} %copy-done.12, bf16[128,128]{1,0:T(8,128)(2,1)} %copy-done.13, ...), custom_call_target="tpu_custom_call" | custom-call | flops 4831838208 | bytes 2097152 | tf_op jit(solution)/shard_map/edges_1/pallas_call | solution.py:252
  87.6 4.2 %nodes_1.1 = bf16[1024,128]{1,0:T(8,128)(2,1)} custom-call(bf16[1024,128]{1,0:T(8,128)(2,1)} %get-tuple-element.24.nodes_ref, bf16[1024,128]{1,0:T(8,128)(2,1)} %get-tuple-element.30.summed_ref, bf16[1024,128]{1,0:T(8,128)(2,1)} %get-tuple-element.31.context_ref, f32[1,128]{1,0:T(1,128)} %get-tuple-element.32.pooled_ref, bf16[2,384,128]{2,1,0:T(8,128)(2,1)} %w_in_ref.7, ...), custom_call_target="tpu_custom_call" | custom-call | tf_op jit(solution)/shard_map/nodes_1/pallas_call | solution.py:486
  (25 shorter events, 0.0 us)
Async XLA Ops:
  18.2 9.4 %copy-start.8 = (bf16[128,128]{1,0:T(8,128)(2,1)S(1)}, bf16[128,128]{1,0:T(8,128)(2,1)}, u32[]{:S(2)}) copy-start(bf16[128,128]{1,0:T(8,128)(2,1)} %get-tuple-element.18) | copy-start | bytes 98308
  18.2 10.7 %copy-start.5 = (bf16[128,128]{1,0:T(8,128)(2,1)S(1)}, bf16[128,128]{1,0:T(8,128)(2,1)}, u32[]{:S(2)}) copy-start(bf16[128,128]{1,0:T(8,128)(2,1)} %get-tuple-element.19) | copy-start | bytes 98308
  18.2 12.6 %copy-start.4 = (bf16[128,128]{1,0:T(8,128)(2,1)S(1)}, bf16[128,128]{1,0:T(8,128)(2,1)}, u32[]{:S(2)}) copy-start(bf16[128,128]{1,0:T(8,128)(2,1)} %get-tuple-element.20) | copy-start | bytes 98308
  18.2 13.4 %copy-start.3 = (bf16[128,128]{1,0:T(8,128)(2,1)S(1)}, bf16[128,128]{1,0:T(8,128)(2,1)}, u32[]{:S(2)}) copy-start(bf16[128,128]{1,0:T(8,128)(2,1)} %get-tuple-element.21) | copy-start | bytes 98308
  18.2 36.5 %all-to-all-start.1 = ((bf16[32,80,128]{2,1,0:T(8,128)(2,1)}), bf16[32,80,128]{2,1,0:T(8,128)(2,1)S(1)}, u32[]{:S(2)}, u32[]{:S(2)}) async-start(bf16[32,80,128]{2,1,0:T(8,128)(2,1)} %middle.1), calls=%async_computation.1 | async-start | bytes 1310720 | tf_op jit(solution)/shard_map/all_to_all | solution.py:409
  27.6 7.0 %copy-start.1 = (f32[2,3,128]{2,0,1:T(2,128)S(1)}, f32[2,3,128]{2,0,1:T(2,128)}, u32[]{:S(2)}) copy-start(f32[2,3,128]{2,0,1:T(2,128)} %param.25) | copy-start | bytes 9220
  27.6 8.2 %collective-permute-start = (bf16[128,128]{1,0:T(8,128)(2,1)S(1)}, bf16[128,128]{1,0:T(8,128)(2,1)S(1)}, u32[]{:S(2)}, u32[]{:S(2)}) collective-permute-start(bf16[128,128]{1,0:T(8,128)(2,1)S(1)} %copy-done.8), channel_id=1, source_target_pairs={{0,32},{32,0},{64,96},{96,64},{128,160},{160,128},{192,224},{224,1... | collective-permute-start | bytes 98312 | tf_op jit(solution)/shard_map/ppermute | solution.py:396
  28.9 6.9 %collective-permute-start.1 = (bf16[128,128]{1,0:T(8,128)(2,1)S(1)}, bf16[128,128]{1,0:T(8,128)(2,1)S(1)}, u32[]{:S(2)}, u32[]{:S(2)}) collective-permute-start(bf16[128,128]{1,0:T(8,128)(2,1)S(1)} %copy-done.5), channel_id=1, source_target_pairs={{32,64},{64,32},{96,128},{128,96},{160,192},{192,160},{33,65},{65,... | collective-permute-start | bytes 98312 | tf_op jit(solution)/shard_map/ppermute | solution.py:396
  30.8 5.0 %collective-permute-start.2 = (bf16[128,128]{1,0:T(8,128)(2,1)S(1)}, bf16[128,128]{1,0:T(8,128)(2,1)S(1)}, u32[]{:S(2)}, u32[]{:S(2)}) collective-permute-start(bf16[128,128]{1,0:T(8,128)(2,1)S(1)} %copy-done.4), channel_id=1, source_target_pairs={{0,1},{1,0},{2,3},{3,2},{4,5},{5,4},{6,7},{7,6},{8,9},{9,8},{10,11... | collective-permute-start | bytes 98312 | tf_op jit(solution)/shard_map/ppermute | solution.py:396
  31.6 3.6 %copy-start.2 = (f32[2,3,128]{2,0,1:T(2,128)S(1)}, f32[2,3,128]{2,0,1:T(2,128)}, u32[]{:S(2)}) copy-start(f32[2,3,128]{2,0,1:T(2,128)} %param.30) | copy-start | bytes 9220
  31.6 7.5 %collective-permute-start.3 = (bf16[128,128]{1,0:T(8,128)(2,1)S(1)}, bf16[128,128]{1,0:T(8,128)(2,1)S(1)}, u32[]{:S(2)}, u32[]{:S(2)}) collective-permute-start(bf16[128,128]{1,0:T(8,128)(2,1)S(1)} %copy-done.3), channel_id=1, source_target_pairs={{1,2},{2,1},{3,4},{4,3},{5,6},{6,5},{7,8},{8,7},{9,10},{10,9},{11,... | collective-permute-start | bytes 98312 | tf_op jit(solution)/shard_map/ppermute | solution.py:396
  35.8 3.3 %copy-start.6 = (bf16[128,128]{1,0:T(8,128)(2,1)}, bf16[128,128]{1,0:T(8,128)(2,1)S(1)}, u32[]{:S(2)}) copy-start(bf16[128,128]{1,0:T(8,128)(2,1)S(1)} %collective-permute-done.halo_a) | copy-start | bytes 98308
  35.8 3.3 %copy-start.9 = (bf16[128,128]{1,0:T(8,128)(2,1)}, bf16[128,128]{1,0:T(8,128)(2,1)S(1)}, u32[]{:S(2)}) copy-start(bf16[128,128]{1,0:T(8,128)(2,1)S(1)} %collective-permute-done.1.halo_b) | copy-start | bytes 98308
  35.8 3.3 %copy-start.11 = (bf16[128,128]{1,0:T(8,128)(2,1)}, bf16[128,128]{1,0:T(8,128)(2,1)S(1)}, u32[]{:S(2)}) copy-start(bf16[128,128]{1,0:T(8,128)(2,1)S(1)} %collective-permute-done.2.halo_c) | copy-start | bytes 98308
  39.1 0.6 copy-start.14
  54.7 0.8 copy-start
  60.7 6.9 %collective-permute-start.4 = (bf16[128,128]{1,0:T(8,128)(2,1)}, bf16[128,128]{1,0:T(8,128)(2,1)S(1)}, u32[]{:S(2)}, u32[]{:S(2)}) collective-permute-start(bf16[128,128]{1,0:T(8,128)(2,1)} %get-tuple-element.25), channel_id=1, source_target_pairs={{0,32},{32,0},{64,96},{96,64},{128,160},{160,128},{192,224},{224,1... | collective-permute-start | bytes 98312 | tf_op jit(solution)/shard_map/ppermute | solution.py:396
  60.9 6.8 %collective-permute-start.5 = (bf16[128,128]{1,0:T(8,128)(2,1)}, bf16[128,128]{1,0:T(8,128)(2,1)S(1)}, u32[]{:S(2)}, u32[]{:S(2)}) collective-permute-start(bf16[128,128]{1,0:T(8,128)(2,1)} %get-tuple-element.26), channel_id=1, source_target_pairs={{32,64},{64,32},{96,128},{128,96},{160,192},{192,160},{33,65},{65,... | collective-permute-start | bytes 98312 | tf_op jit(solution)/shard_map/ppermute | solution.py:396
  64.3 3.3 %collective-permute-start.6 = (bf16[128,128]{1,0:T(8,128)(2,1)}, bf16[128,128]{1,0:T(8,128)(2,1)S(1)}, u32[]{:S(2)}, u32[]{:S(2)}) collective-permute-start(bf16[128,128]{1,0:T(8,128)(2,1)} %get-tuple-element.27), channel_id=1, source_target_pairs={{0,1},{1,0},{2,3},{3,2},{4,5},{5,4},{6,7},{7,6},{8,9},{9,8},{10,11... | collective-permute-start | bytes 98312 | tf_op jit(solution)/shard_map/ppermute | solution.py:396
  64.4 7.6 %collective-permute-start.7 = (bf16[128,128]{1,0:T(8,128)(2,1)}, bf16[128,128]{1,0:T(8,128)(2,1)S(1)}, u32[]{:S(2)}, u32[]{:S(2)}) collective-permute-start(bf16[128,128]{1,0:T(8,128)(2,1)} %get-tuple-element.28), channel_id=1, source_target_pairs={{1,2},{2,1},{3,4},{4,3},{5,6},{6,5},{7,8},{8,7},{9,10},{10,9},{11,... | collective-permute-start | bytes 98312 | tf_op jit(solution)/shard_map/ppermute | solution.py:396
  67.6 4.4 %copy-start.7 = (bf16[128,128]{1,0:T(8,128)(2,1)}, bf16[128,128]{1,0:T(8,128)(2,1)S(1)}, u32[]{:S(2)}) copy-start(bf16[128,128]{1,0:T(8,128)(2,1)S(1)} %collective-permute-done.4.halo_a) | copy-start | bytes 98308
  67.6 4.4 %copy-start.10 = (bf16[128,128]{1,0:T(8,128)(2,1)}, bf16[128,128]{1,0:T(8,128)(2,1)S(1)}, u32[]{:S(2)}) copy-start(bf16[128,128]{1,0:T(8,128)(2,1)S(1)} %collective-permute-done.5.halo_b) | copy-start | bytes 98308
  67.6 4.3 %copy-start.12 = (bf16[128,128]{1,0:T(8,128)(2,1)}, bf16[128,128]{1,0:T(8,128)(2,1)S(1)}, u32[]{:S(2)}) copy-start(bf16[128,128]{1,0:T(8,128)(2,1)S(1)} %collective-permute-done.6.halo_c) | copy-start | bytes 98308
  72.0 0.6 copy-start.13

commit v2 on v1

v2 whole, which is shorter than its diff:
```python
import functools
import math

import jax
import jax.numpy as jnp
from jax import lax
from jax.experimental import pallas as pl
from jax.experimental.pallas import tpu as pltpu
from jax.sharding import Mesh
from jax.sharding import PartitionSpec as P


LAYERS = 2
COL = ("col_0", "col_1", "col_2")
ROW_COL = ("row", "col_0", "col_1", "col_2")
EPS = 1e-05
W = 128
TILE = 1024
BF = jnp.bfloat16
F32 = jnp.float32
VM = pltpu.VMEM
VMEM_LIMIT = 66_600_960


def dot(a, b):
    return jnp.dot(a, b, preferred_element_type=F32)


def columns(stack, count):
    turned = jnp.transpose(stack)
    return [
        jnp.broadcast_to(turned[:, k : k + 1], (W, W)).astype(jnp.int16) for k in range(count)
    ]


def column_hot(col, count):
    lane = lax.broadcasted_iota(jnp.int16, (1, W), 1)
    one, zero = jnp.ones((), BF), jnp.zeros((), BF)
    pieces = [
        jnp.where(col == lane + jnp.int16(W * c), one, zero) for c in range(count // W)
    ]
    return jnp.concatenate(pieces, axis=1)


def row_hot(row, count):
    spread = jnp.broadcast_to(row, (16, W)).astype(jnp.int16)
    at = lax.broadcasted_iota(jnp.int16, (16, W), 0)
    one, zero = jnp.ones((), BF), jnp.zeros((), BF)
    pieces = [jnp.where(spread == at + jnp.int16(16 * c), one, zero) for c in range(count // 16)]
    return jnp.concatenate(pieces, axis=0)


def split2(value):
    high = value.astype(BF)
    low = (value - high.astype(F32)).astype(BF)
    return high, low


def split3(value):
    high = value.astype(BF)
    rest = value - high.astype(F32)
    mid = rest.astype(BF)
    low = (rest - mid.astype(F32)).astype(BF)
    return high, mid, low


def centred_weights(w_out, b_out):
    full = w_out.astype(F32)
    full = full - jnp.mean(full, axis=1, keepdims=True)
    high, low = split2(full)
    return jnp.concatenate([high, low], axis=1), b_out - jnp.mean(b_out, axis=1, keepdims=True)


def norm_tail(pre, w_two, b_centred, gain, shift):
    hidden = jnp.maximum(pre, 0.0).astype(BF)
    both = dot(hidden, w_two)
    centred = both[:, :W] + both[:, W:] + b_centred
    spread = jnp.mean(centred * centred, axis=-1, keepdims=True)
    return centred * lax.rsqrt(spread + EPS) * gain + shift


def picked_rows(table_two, half_rows, col):
    hot = column_hot(col & jnp.int16(half_rows - 1), half_rows)
    both = dot(hot, table_two)
    upper = col.astype(jnp.int32) >= half_rows
    return jnp.where(upper, both[:, W:], both[:, :W]).astype(BF)


def phases(first, second, odd):
    return jnp.where(odd, second, first), jnp.where(odd, first, second)


def start_kernel(nodes_ref, send_ref, context_ref, payload_ref, pick_col, *picked_refs):
    nodes = nodes_ref[...]
    half = nodes.shape[0] // 2
    two = jnp.concatenate([nodes[:half], nodes[half:]], axis=1)
    row_odd = lax.rem(lax.axis_index("row"), 2) == 1
    col_odd = lax.axis_index("col_2") == 1
    index = [send_ref[0, k : k + 1, :] for k in range(4)]
    index_a, index_b = phases(index[0], index[1], row_odd)
    index_c, index_d = phases(index[2], index[3], col_odd)
    stack = jnp.concatenate([index_a, index_b, index_c, index_d] + [index_a] * 4, axis=0)
    col = jnp.concatenate(columns(stack, 4), axis=0)
    pick_col[...] = col
    picked = picked_rows(two, half, col)
    for k, ref in enumerate(picked_refs):
        ref[...] = picked[W * k : W * (k + 1)]
    local_sum = jnp.sum(nodes.astype(F32), axis=0, keepdims=True)
    block = jnp.concatenate(
        [context_ref[...].astype(F32)]
        + [p.astype(F32) for p in split3(local_sum)]
        + [jnp.zeros((5, W), F32)],
        axis=0,
    ).astype(BF)
    for k in range(payload_ref.shape[0]):
        payload_ref[k] = block


def middle_kernel(got_ref, payload_ref):
    got = [got_ref[k].astype(F32) for k in range(got_ref.shape[0])]
    total = functools.reduce(
        lambda a, b: a + b, [g[8:9] + (g[9:10] + g[10:11]) for g in got]
    )
    high, mid, low = split3(total)
    block = jnp.concatenate(
        [g[:8] for g in got]
        + [high.astype(F32), mid.astype(F32), low.astype(F32), jnp.zeros((13, W), F32)],
        axis=0,
    ).astype(BF)
    for k in range(payload_ref.shape[0]):
        payload_ref[k] = block


def project(nodes, halo, w_in, send_table, recv_table):
    node_count = nodes.shape[0]
    send_half, recv_half = (node_count + 4 * W) // 2, node_count // 2
    ext = jnp.concatenate([nodes, *halo], axis=0)
    from_send = dot(ext, w_in[:W]).astype(BF)
    from_recv = dot(nodes, w_in[W : 2 * W]).astype(BF)
    send_table[:send_half, :W] = from_send[:send_half]
    send_table[:send_half, W:] = from_send[send_half:]
    send_table[send_half:, :W] = w_in[2 * W :]
    send_table[send_half:, W:] = w_in[2 * W :]
    recv_table[:, :W] = from_recv[:recv_half]
    recv_table[:, W:] = from_recv[recv_half:]


def edge_pre(edges, send16, recv16, send_table, recv_table, bias):
    recv_half = recv_table.shape[0]
    send_half = send_table.shape[0] - W
    send_local = jnp.where(send16 >= jnp.int16(send_half), send16 - jnp.int16(send_half), send16)
    send_hot = column_hot(send_local, send_half)
    recv_hot = column_hot(recv16 & jnp.int16(recv_half - 1), recv_half)
    both_s = dot(jnp.concatenate([send_hot, edges], axis=1), send_table[...])
    both_r = dot(recv_hot, recv_table[...])
    upper_s = send16.astype(jnp.int32) >= send_half
    upper_r = recv16.astype(jnp.int32) >= recv_half
    return (
        jnp.where(upper_s, both_s[:, W:], both_s[:, :W])
        + jnp.where(upper_r, both_r[:, W:], both_r[:, :W])
        + bias
    )


def edge_tail(pre, edges, recv16, recv_rows, recv_half, w_two, biases, gain):
    tail = norm_tail(pre, w_two, biases[1], gain, biases[2])
    fresh = (edges.astype(F32) + tail).astype(BF)
    lower16 = recv16 < jnp.int16(recv_half)
    zero = jnp.zeros((), BF)
    fresh_two = jnp.concatenate(
        [jnp.where(lower16, fresh, zero), jnp.where(lower16, zero, fresh)], axis=1
    )
    rows = recv_rows & (recv_half - 1)
    turned = jnp.concatenate(
        [row_hot(rows[k : k + 1], recv_half) for k in range(rows.shape[0])], axis=1
    )
    return fresh, dot(turned, fresh_two)


def edge_kernel(layer, last, *refs):
    nodes_ref, *refs = refs
    halo, refs = refs[:4], refs[4:]
    (send_hbm, recv_hbm, receivers_ref, edges_hbm, w_in_ref, w_out_ref, bias_ref, gain_ref), refs = (
        refs[:8],
        refs[8:],
    )
    if last:
        node_refs, refs = refs[:7], refs[7:]
    fresh_hbm, node_side, *refs = refs
    send_table, recv_table, acc, w_two, even_pre, odd_pre, *refs = refs
    send_col, recv_col, edges_ref, fresh_buf, in_sems, out_sems = refs
    recv_half = nodes_ref.shape[0] // 2
    steps = edges_ref.shape[0] // TILE
    per = TILE // W

    def strip(i):
        start = i * TILE
        return pl.ds(start if isinstance(i, int) else pl.multiple_of(start, TILE), TILE)

    def in_copies(i):
        at = strip(i)
        return [
            pltpu.make_async_copy(hbm.at[at], ref.at[at], in_sems.at[k, i])
            for k, (hbm, ref) in enumerate(
                ((send_hbm, send_col), (recv_hbm, recv_col), (edges_hbm, edges_ref))
            )
        ]

    def out_copy(i):
        at = strip(i)
        return pltpu.make_async_copy(fresh_buf.at[at], fresh_hbm.at[at], out_sems.at[i])

    for i in range(steps):
        for copy in in_copies(i):
            copy.start()

    project(nodes_ref[...], [h[...] for h in halo], w_in_ref[0], send_table, recv_table)
    two, b_centred = centred_weights(w_out_ref[0], bias_ref[1, layer : layer + 1])
    w_two[...] = two
    acc[...] = jnp.zeros_like(acc)
    biases = (bias_ref[0, layer : layer + 1], b_centred, bias_ref[2, layer : layer + 1])
    gain = gain_ref[layer : layer + 1]

    def arrive(i):
        for copy in in_copies(i):
            copy.wait()

    def pre_of(i):
        at = strip(i)
        return edge_pre(
            edges_ref[at], send_col[at], recv_col[at], send_table, recv_table, biases[0]
        )

    def tail_of(i, pre):
        at = strip(i)
        rows = receivers_ref[pl.ds(i * per, per)]
        return edge_tail(
            pre, edges_ref[at], recv_col[at], rows, recv_half, w_two[...], biases, gain
        )

    def both(i, now, later):
        arrive(i + 1)
        pre = pre_of(i + 1)
        fresh, added = tail_of(i, now[...])
        later[...] = pre
        acc[...] += added
        fresh_buf[strip(i)] = fresh
        out_copy(i).start()

    arrive(0)
    even_pre[...] = pre_of(0)

    def body(j, carry):
        both(2 * j, even_pre, odd_pre)
        both(2 * j + 1, odd_pre, even_pre)
        return carry

    lax.fori_loop(0, steps // 2 - 1, body, 0)
    both(steps - 2, even_pre, odd_pre)
    fresh, added = tail_of(steps - 1, odd_pre[...])
    fresh_buf[strip(steps - 1)] = fresh
    out_copy(steps - 1).start()
    sums = acc[...] + added
    summed = jnp.concatenate([sums[:, :W], sums[:, W:]], axis=0).astype(BF)
    if last:
        context_ref, pooled_ref, *weights = node_refs
        node_side[...] = node_update(
            layer, nodes_ref[...], summed, context_ref[...], pooled_ref[...], *weights
        )
    else:
        node_side[...] = summed

    def drain(i, carry):
        out_copy(i).wait()
        return carry

    lax.fori_loop(0, steps, drain, 0)


def params():
    return pltpu.CompilerParams(vmem_limit_bytes=VMEM_LIMIT)


def whole(arg):
    return pl.BlockSpec(arg.shape, lambda i: (0,) * len(arg.shape))


def of_layer(arg, layer):
    if arg.ndim != 3 or arg.shape[0] != LAYERS:
        return whole(arg)
    return pl.BlockSpec((1, *arg.shape[1:]), lambda i: (layer, 0, 0))


def edge_step(layer, last, nodes, halo, send_col, recv_col, receivers, edges, weights, node_args):
    node_count, edge_count = nodes.shape[0], edges.shape[0]
    half, ext_half = node_count // 2, (node_count + 4 * W) // 2
    flops = 2 * edge_count * W * (2 * ext_half + 4 * half + 8 * W)
    args = [nodes, *halo, send_col, recv_col, receivers, edges, *weights, *node_args]
    specs = [of_layer(arg, layer) for arg in args]
    for k in (1, 2, 3, 4):
        specs[k] = pl.BlockSpec(memory_space=VM)
    for k in (5, 6, 8):
        specs[k] = pl.BlockSpec(memory_space=pltpu.HBM)
    steps = edge_count // TILE
    return pl.pallas_call(
        functools.partial(edge_kernel, layer, last),
        grid=(1,),
        in_specs=specs,
        out_specs=[pl.BlockSpec(memory_space=pltpu.HBM), whole(nodes)],
        out_shape=[
            jax.ShapeDtypeStruct(edges.shape, BF),
            jax.ShapeDtypeStruct(nodes.shape, BF),
        ],
        scratch_shapes=[
            VM((ext_half + W, 2 * W), BF),
            VM((half, 2 * W), BF),
            VM((half, 2 * W), F32),
            VM((W, 2 * W), BF),
            VM((TILE, W), F32),
            VM((TILE, W), F32),
            VM((edge_count, W), jnp.int16),
            VM((edge_count, W), jnp.int16),
            VM(edges.shape, BF),
            VM(edges.shape, BF),
            pltpu.SemaphoreType.DMA((3, steps)),
            pltpu.SemaphoreType.DMA((steps,)),
        ],
        compiler_params=params(),
        cost_estimate=pl.CostEstimate(
            flops=flops, bytes_accessed=4 * edge_count * W, transcendentals=0
        ),
    )(*args)


def node_update(layer, nodes, summed, context, pooled, w_in_ref, wg_ref, w_out_ref, bias_ref, gain_ref):
    parts = jnp.concatenate(
        [p.astype(F32) for p in split3(pooled)] + [jnp.zeros((13, W), F32)], axis=0
    ).astype(BF)
    through = dot(parts, wg_ref[0])
    shift_in = bias_ref[0, layer : layer + 1] + (through[0:1] + (through[1:2] + through[2:3]))
    w_two, b_centred = centred_weights(w_out_ref[0], bias_ref[1, layer : layer + 1])
    feats = jnp.concatenate([nodes, summed, context], axis=1)
    pre = dot(feats, w_in_ref[0]) + shift_in
    tail = norm_tail(
        pre, w_two, b_centred, gain_ref[layer : layer + 1], bias_ref[2, layer : layer + 1]
    )
    return (nodes.astype(F32) + tail).astype(BF)


def prepare_kernel(senders_ref, receivers_ref, region_ref, send_col, recv_col, region_col):
    node_count = region_ref.shape[0] * W
    senders = senders_ref[...]
    row_flip = jnp.where(lax.rem(lax.axis_index("row"), 2) == 1, 0, W)
    col_flip = jnp.where(lax.axis_index("col_2") == 1, 0, W)
    flip = jnp.where(senders < node_count + 2 * W, row_flip, col_flip)
    senders = jnp.where(senders < node_count, senders, senders ^ flip)
    region = region_ref[...]
    place = ((region >> 3) & 31) * 64 + (region >> 8) * 8 + (region & 7)
    for values, ref in (
        (senders, send_col),
        (receivers_ref[...], recv_col),
        (place, region_col),
    ):
        for k, block in enumerate(columns(values, values.shape[0])):
            ref[W * k : W * (k + 1)] = block


def first_node_kernel(
    nodes_ref,
    summed_ref,
    table_ref,
    region_col,
    pick_col,
    w_in_ref,
    wg_ref,
    w_out_ref,
    bias_ref,
    gain_ref,
    nodes_out,
    context_out,
    pooled_out,
    a_out,
    b_out,
    c_out,
    d_out,
    table_two,
    fresh_two,
):
    groups, _, _ = table_ref.shape
    own = 8 * 8
    half_groups = groups // 2
    half = half_groups * own
    total = jnp.zeros((1, W), F32)
    for g in range(groups):
        top = own * (g % half_groups)
        side = W * (g // half_groups)
        table_two[top : top + own, side : side + W] = table_ref[g, :own]
        tail = table_ref[g, own : own + 16].astype(F32)
        total = total + (tail[0:1] + (tail[1:2] + tail[2:3]))
    node_count = nodes_ref.shape[0]
    everyone = node_count * 8 * groups
    pooled = total / math.sqrt(everyone)
    pooled_out[...] = pooled
    node_half = node_count // 2
    context = picked_rows(table_two[...], half, region_col[...])
    context_out[...] = context
    fresh = node_update(
        0,
        nodes_ref[...],
        summed_ref[...],
        context,
        pooled,
        w_in_ref,
        wg_ref,
        w_out_ref,
        bias_ref,
        gain_ref,
    )
    nodes_out[...] = fresh
    fresh_two[:, :W] = fresh[:node_half]
    fresh_two[:, W:] = fresh[node_half:]
    picked = picked_rows(fresh_two[...], node_half, pick_col[...])
    for k, ref in enumerate((a_out, b_out, c_out, d_out)):
        ref[...] = picked[W * k : W * (k + 1)]


def exchanged(block, axis, phase):
    devices = lax.axis_size(axis)
    pairs = []
    for i in range(phase, devices - 1, 2):
        pairs += [(i, i + 1), (i + 1, i)]
    return lax.ppermute(block, axis, pairs)


def halo_of(picked):
    halo = []
    for k, (axis, phase) in enumerate((("row", 0), ("row", 1), (COL, 0), (COL, 1))):
        halo.append(exchanged(picked[k], axis, phase))
    return halo


def to_everyone(copies, axis):
    return lax.all_to_all(copies, axis, split_axis=0, concat_axis=0, tiled=True)


def local(
    node_latent,
    edge_latent,
    senders,
    receivers,
    send_index,
    context_table,
    region,
    edge_w1,
    edge_w2,
    edge_bias,
    edge_gain,
    node_w1,
    node_wg,
    node_w2,
    node_bias,
    node_gain,
):
    n_row, n_col = lax.axis_size("row"), lax.axis_size(COL)
    node_count, edge_count = node_latent.shape[0], edge_latent.shape[0]
    senders, receivers, region = (v.reshape(-1, W) for v in (senders, receivers, region))
    edge_bias, node_bias = (v.transpose(1, 0, 2) for v in (edge_bias, node_bias))
    block = jax.ShapeDtypeStruct((W, W), BF)
    column = lambda rows: jax.ShapeDtypeStruct((rows, W), jnp.int16)
    payload, pick_col, *picked = pl.pallas_call(
        start_kernel,
        out_shape=[jax.ShapeDtypeStruct((n_row, 16, W), BF), column(4 * W)] + [block] * 4,
        compiler_params=params(),
        name="start",
    )(node_latent, send_index, context_table)
    by_row = to_everyone(payload, "row")
    halo = halo_of(picked)
    send_col, recv_col, region_col = pl.pallas_call(
        prepare_kernel,
        out_shape=[column(edge_count), column(edge_count), column(node_count)],
        compiler_params=params(),
        cost_estimate=pl.CostEstimate(
            flops=2 * edge_count * W * W * 4, bytes_accessed=4 * edge_count * W, transcendentals=0
        ),
        name="prepare",
    )(senders, receivers, region)
    by_row, *halo = lax.optimization_barrier((by_row, *halo))
    second = pl.pallas_call(
        middle_kernel,
        in_specs=[pl.BlockSpec(memory_space=VM)],
        out_specs=pl.BlockSpec(memory_space=VM),
        out_shape=jax.ShapeDtypeStruct((n_col, 80, W), BF),
        compiler_params=pltpu.CompilerParams(vmem_limit_bytes=8 << 20),
        name="middle",
    )(by_row)
    table = to_everyone(second, COL)
    weights = (edge_w1, edge_w2, edge_bias, edge_gain)
    node_weights = (node_w1, node_wg, node_w2, node_bias, node_gain)
    edges, summed = edge_step(
        0, False, node_latent, halo, send_col, recv_col, receivers, edge_latent, weights, ()
    )
    node_outs = (
        [jax.ShapeDtypeStruct(node_latent.shape, BF)] * 2
        + [jax.ShapeDtypeStruct((1, W), F32)]
        + [block] * 4
    )
    nodes, context, pooled, *picked = pl.pallas_call(
        first_node_kernel,
        grid=(1,),
        in_specs=[
            of_layer(v, 0) for v in (node_latent, summed, table, region_col, pick_col, *node_weights)
        ],
        out_specs=[whole(v) for v in node_outs],
        out_shape=node_outs,
        scratch_shapes=[
            VM((n_col // 2 * 64, 2 * W), BF),
            VM((node_count // 2, 2 * W), BF),
        ],
        compiler_params=params(),
        name="nodes_0",
    )(node_latent, summed, table, region_col, pick_col, *node_weights)
    halo = halo_of(picked)
    edges, nodes = edge_step(
        1,
        True,
        nodes,
        halo,
        send_col,
        recv_col,
        receivers,
        edges,
        weights,
        (context, pooled, *node_weights),
    )
    return (nodes, edges)


def solution(mesh):
    finer = Mesh(
        mesh.devices.reshape(mesh.shape["row"], 4, 4, 2), ("row", "col_0", "col_1", "col_2")
    )
    placed = (
        P(ROW_COL, None),
        P(ROW_COL, None),
        P(ROW_COL),
        P(ROW_COL),
        P(ROW_COL, None, None),
        P(ROW_COL, None),
        P(ROW_COL),
        P(),
        P(),
        P(),
        P(),
        P(),
        P(),
        P(),
        P(),
        P(),
    )
    return jax.shard_map(
        local,
        mesh=finer,
        in_specs=placed,
        out_specs=(P(ROW_COL, None), P(ROW_COL, None)),
        check_vma=False,
    )
```

time: 92.5 us -> 76.3 us (0.82)
  blocking collectives: 13.8 us -> 0 us
  Pallas kernels: 43.1 us -> 32.4 us
  starting transfers between devices: 23.3 us -> 33.2 us
  local copies, waits for them, and re-layouts: 3.22 us -> 0.63 us
  waiting for transfers between devices: 7.57 us -> 8.52 us
    all_to_all x1 -> x0, blocking collectives: 13.8 us -> none  [to_everyone(): return lax.all_to_all(copies, axis, split_axis=0, concat_axis=0, tiled=True)]
    pallas_call x5, Pallas kernels: 41 us -> 30.3 us  [the longest x2 21.8 us: edge_step(): pl.pallas_call(functools.partial(edge_kernel, layer, last), grid=(1,), in...]
    all_to_all x1 -> x2, starting transfers between devices: 9.42 us -> 15.2 us  [to_everyone(): return lax.all_to_all(copies, axis, split_axis=0, concat_axis=0, tiled=True)]
    ppermute x8, starting transfers between devices: 13.8 us -> 18 us  [exchanged(): return lax.ppermute(block, axis, pairs)]
    unnamed x32 -> x20, local copies, waits for them, and re-layouts: 3.22 us -> 0.63 us
    ppermute x8, waiting for transfers between devices: 7.57 us -> 8.52 us  [exchanged(): return lax.ppermute(block, axis, pairs)]
  transfers between devices with their start and end apart: 9 -> 10, of which waited for: 2 -> 2; matrix products, arithmetic and copies ran while one was open for 1% -> 0% of each run, Pallas kernels for 16% -> 18%
where the time goes in v2:
time: 76.3 us; the launch traced here: 75.8 us
  starting transfers between devices  33.2 us (44%)
  Pallas kernels  32.4 us (42%)
  waiting for transfers between devices  8.52 us (11%)
  between operations  0.99 us (1%)
    pallas_call x2, Pallas kernels, edge_step(): pl.pallas_call(functools.partial(edge_kernel, layer, last), grid=(1,), in...  21.8 us
    ppermute x8, starting transfers between devices, exchanged(): return lax.ppermute(block, axis, pairs)  18 us
    all_to_all x2, starting transfers between devices, to_everyone(): return lax.all_to_all(copies, axis, split_axis=0, concat_axis=0, tiled=True)  15.2 us
    ppermute x8, waiting for transfers between devices, exchanged(): return lax.ppermute(block, axis, pairs)  8.52 us
    pallas_call x1, Pallas kernels, local(): pl.pallas_call(first_node_kernel, grid=(1,), in_specs=[of_layer(v, 0) for...  4.17 us
    pallas_call x1, Pallas kernels, local(): pl.pallas_call(prepare_kernel, out_shape=[column(edge_count), column(edge...  3.46 us
    pallas_call x1, Pallas kernels, local(): pl.pallas_call(start_kernel, out_shape=[jax.ShapeDtypeStruct((n_row, 16,...  2.06 us
  transfers between devices with their start and end apart: 10, of which 2 were waited for; matrix products, arithmetic and copies ran while one was open for 0% of the time, Pallas kernels for 18%

profile of v2, /device:TPU:39, one launch (start us, length us, event | category | flops | bytes accessed | tf_op | source)
XLA Modules:
  0.0 75.8 jit_solution(11325432541594711893)
XLA Ops:
  0.6 2.1 %start.1 = (bf16[8,16,128]{2,1,0:T(8,128)(2,1)}, s16[512,128]{1,0:T(8,128)(2,1)}, bf16[128,128]{1,0:T(8,128)(2,1)}, bf16[128,128]{1,0:T(8,128)(2,1)}, bf16[128,1...) custom-call(bf16[1024,128]{1,0:T(8,128)(2,1)} %nodes_ref.3, s32[1,4,128]{2,1,0:T(4,128)} %send_ref.1, bf16[8,128]{1,0:T(8,128)(2,1)} %context_ref.1), custom_call_target="tpu_custom_call" | custom-call | tf_op jit(solution)/shard_map/start/pallas_call | solution.py:470
  2.7 8.1 %all-to-all-start = ((bf16[8,16,128]{2,1,0:T(8,128)(2,1)}), bf16[8,16,128]{2,1,0:T(8,128)(2,1)S(1)}, u32[]{:S(2)}, u32[]{:S(2)}) async-start(bf16[8,16,128]{2,1,0:T(8,128)(2,1)} %get-tuple-element.27), calls=%async_computation | async-start | bytes 65536 | tf_op jit(solution)/shard_map/all_to_all | solution.py:443
  10.8 0.0 collective-permute-start
  10.9 4.2 %collective-permute-start.1 = (bf16[128,128]{1,0:T(8,128)(2,1)}, bf16[128,128]{1,0:T(8,128)(2,1)S(1)}, u32[]{:S(2)}, u32[]{:S(2)}) collective-permute-start(bf16[128,128]{1,0:T(8,128)(2,1)} %get-tuple-element.29), channel_id=1, source_target_pairs={{32,64},{64,32},{96,128},{128,96},{160,192},{192,160},{33,65},{65,... | collective-permute-start | bytes 98312 | tf_op jit(solution)/shard_map/ppermute | solution.py:432
  15.1 0.0 copy-done.7
  15.1 1.9 %collective-permute-start.2 = (bf16[128,128]{1,0:T(8,128)(2,1)S(1)}, bf16[128,128]{1,0:T(8,128)(2,1)S(1)}, u32[]{:S(2)}, u32[]{:S(2)}) collective-permute-start(bf16[128,128]{1,0:T(8,128)(2,1)S(1)} %copy-done.7), channel_id=1, source_target_pairs={{0,1},{1,0},{2,3},{3,2},{4,5},{5,4},{6,7},{7,6},{8,9},{9,8},{10,11... | collective-permute-start | bytes 98312 | tf_op jit(solution)/shard_map/ppermute | solution.py:432
  17.0 0.0 copy-done.5
  17.0 3.0 %collective-permute-start.3 = (bf16[128,128]{1,0:T(8,128)(2,1)S(1)}, bf16[128,128]{1,0:T(8,128)(2,1)S(1)}, u32[]{:S(2)}, u32[]{:S(2)}) collective-permute-start(bf16[128,128]{1,0:T(8,128)(2,1)S(1)} %copy-done.5), channel_id=1, source_target_pairs={{1,2},{2,1},{3,4},{4,3},{5,6},{6,5},{7,8},{8,7},{9,10},{10,9},{11,... | collective-permute-start | bytes 98312 | tf_op jit(solution)/shard_map/ppermute | solution.py:432
  20.0 0.0 collective-permute-done.refs_1_
  20.0 0.0 copy-start
  20.1 0.0 collective-permute-done.1.refs_2_
  20.1 0.0 collective-permute-done.2.refs_3_
  20.1 4.2 %collective-permute-done.3.refs_4_ = bf16[128,128]{1,0:T(8,128)(2,1)S(1)} collective-permute-done((bf16[128,128]{1,0:T(8,128)(2,1)S(1)}, bf16[128,128]{1,0:T(8,128)(2,1)S(1)}, u32[]{:S(2)}, u32[]{:S(2)}) %collective-permute-start.3) | collective-permute-done | bytes 32800 | tf_op jit(solution)/shard_map/ppermute | solution.py:432
  24.3 0.0 all-to-all-done.got_ref
  24.3 0.9 %middle.1 = bf16[32,80,128]{2,1,0:T(8,128)(2,1)} custom-call(bf16[8,16,128]{2,1,0:T(8,128)(2,1)S(1)} %all-to-all-done.got_ref), custom_call_target="tpu_custom_call" | custom-call | tf_op jit(solution)/shard_map/middle/pallas_call | solution.py:488
  25.3 7.1 %all-to-all-start.1 = ((bf16[32,80,128]{2,1,0:T(8,128)(2,1)}), bf16[32,80,128]{2,1,0:T(8,128)(2,1)}, u32[]{:S(2)}, u32[]{:S(2)}) async-start(bf16[32,80,128]{2,1,0:T(8,128)(2,1)} %middle.1), calls=%async_computation.1 | async-start | bytes 1310720 | tf_op jit(solution)/shard_map/all_to_all | solution.py:443
  32.4 3.5 %prepare.1 = (s16[4096,128]{1,0:T(8,128)(2,1)}, s16[4096,128]{1,0:T(8,128)(2,1)}, s16[1024,128]{1,0:T(8,128)(2,1)}) custom-call(s32[32,128]{1,0:T(8,128)} %bitcast.7, s32[32,128]{1,0:T(8,128)} %bitcast.8, s32[8,128]{1,0:T(8,128)} %bitcast.11), custom_call_target="tpu_custom_call" | custom-call | flops 536870912 | bytes 2097152 | tf_op jit(solution)/shard_map/prepare/pallas_call | solution.py:478
  35.8 10.5 %shard_map.167 = (bf16[4096,128]{1,0:T(8,128)(2,1)}, bf16[1024,128]{1,0:T(8,128)(2,1)}) custom-call(bf16[1024,128]{1,0:T(8,128)(2,1)} %nodes_ref.3, bf16[128,128]{1,0:T(8,128)(2,1)} %copy-done, bf16[128,128]{1,0:T(8,128)(2,1)} %copy-done.1, bf16[128,128]{1,0:T(8,128)(2,1)} %copy-done.2, bf16[128,128]{1,0:T(8,128)(2,1)} %copy-done.4, ...), custom_call_target="tpu_custom_call" | custom-call | flops 4831838208 | bytes 2097152 | tf_op jit(solution)/shard_map/pallas_call | solution.py:305
  46.4 0.0 all-to-all-done.1.table_ref
  46.4 4.2 %nodes_0.1 = (bf16[1024,128]{1,0:T(8,128)(2,1)}, bf16[1024,128]{1,0:T(8,128)(2,1)}, f32[1,128]{1,0:T(1,128)}, bf16[128,128]{1,0:T(8,128)(2,1)}, bf16[128,128]{1,...) custom-call(bf16[1024,128]{1,0:T(8,128)(2,1)} %nodes_ref.3, ...), custom_call_target="tpu_custom_call" | custom-call | tf_op jit(solution)/shard_map/nodes_0/pallas_call | solution.py:507
  50.6 0.0 collective-permute-start.4
  50.6 4.6 %collective-permute-start.5 = (bf16[128,128]{1,0:T(8,128)(2,1)}, bf16[128,128]{1,0:T(8,128)(2,1)S(1)}, u32[]{:S(2)}, u32[]{:S(2)}) collective-permute-start(bf16[128,128]{1,0:T(8,128)(2,1)} %get-tuple-element.44), channel_id=1, source_target_pairs={{32,64},{64,32},{96,128},{128,96},{160,192},{192,160},{33,65},{65,... | collective-permute-start | bytes 98312 | tf_op jit(solution)/shard_map/ppermute | solution.py:432
  55.2 1.0 %collective-permute-start.6 = (bf16[128,128]{1,0:T(8,128)(2,1)}, bf16[128,128]{1,0:T(8,128)(2,1)S(1)}, u32[]{:S(2)}, u32[]{:S(2)}) collective-permute-start(bf16[128,128]{1,0:T(8,128)(2,1)} %get-tuple-element.45), channel_id=1, source_target_pairs={{0,1},{1,0},{2,3},{3,2},{4,5},{5,4},{6,7},{7,6},{8,9},{9,8},{10,11... | collective-permute-start | bytes 98312 | tf_op jit(solution)/shard_map/ppermute | solution.py:432
  56.2 3.2 %collective-permute-start.7 = (bf16[128,128]{1,0:T(8,128)(2,1)}, bf16[128,128]{1,0:T(8,128)(2,1)S(1)}, u32[]{:S(2)}, u32[]{:S(2)}) collective-permute-start(bf16[128,128]{1,0:T(8,128)(2,1)} %get-tuple-element.46), channel_id=1, source_target_pairs={{1,2},{2,1},{3,4},{4,3},{5,6},{6,5},{7,8},{8,7},{9,10},{10,9},{11,... | collective-permute-start | bytes 98312 | tf_op jit(solution)/shard_map/ppermute | solution.py:432
  59.4 0.0 collective-permute-done.4.refs_1_
  59.4 0.0 collective-permute-done.5.refs_2_
  59.5 0.0 collective-permute-done.6.refs_3_
  59.5 0.0 copy-start.8
  59.5 4.3 %collective-permute-done.7.refs_4_ = bf16[128,128]{1,0:T(8,128)(2,1)S(1)} collective-permute-done((bf16[128,128]{1,0:T(8,128)(2,1)}, bf16[128,128]{1,0:T(8,128)(2,1)S(1)}, u32[]{:S(2)}, u32[]{:S(2)}) %collective-permute-start.7) | collective-permute-done | bytes 32800 | tf_op jit(solution)/shard_map/ppermute | solution.py:432
  63.8 0.0 copy-done.6
  63.8 0.6 copy-done.9
  64.4 11.2 %shard_map.168 = (bf16[4096,128]{1,0:T(8,128)(2,1)}, bf16[1024,128]{1,0:T(8,128)(2,1)}) custom-call(bf16[1024,128]{1,0:T(8,128)(2,1)} %get-tuple-element.42.refs_0_, bf16[128,128]{1,0:T(8,128)(2,1)} %copy-done.3, bf16[128,128]{1,0:T(8,128)(2,1)} %copy-done.6, bf16[128,128]{1,0:T(8,128)(2,1)} %copy-done.8, bf16[128,128]{1,0:T(8,128)(2,1)} %copy-done.9, ...), custom_call_target="tpu_custom_call" | custom-call | flops 4831838208 | bytes 2097152 | tf_op jit(solution)/shard_map/pallas_call | solution.py:305
  (14 shorter events, 0.0 us)
Async XLA Ops:
  2.7 12.4 %copy-start.7 = (bf16[128,128]{1,0:T(8,128)(2,1)S(1)}, bf16[128,128]{1,0:T(8,128)(2,1)}, u32[]{:S(2)}) copy-start(bf16[128,128]{1,0:T(8,128)(2,1)} %get-tuple-element.30) | copy-start | bytes 98308
  2.7 14.3 %copy-start.5 = (bf16[128,128]{1,0:T(8,128)(2,1)S(1)}, bf16[128,128]{1,0:T(8,128)(2,1)}, u32[]{:S(2)}) copy-start(bf16[128,128]{1,0:T(8,128)(2,1)} %get-tuple-element.31) | copy-start | bytes 98308
  2.7 21.6 %all-to-all-start = ((bf16[8,16,128]{2,1,0:T(8,128)(2,1)}), bf16[8,16,128]{2,1,0:T(8,128)(2,1)S(1)}, u32[]{:S(2)}, u32[]{:S(2)}) async-start(bf16[8,16,128]{2,1,0:T(8,128)(2,1)} %get-tuple-element.27), calls=%async_computation | async-start | bytes 65536 | tf_op jit(solution)/shard_map/all_to_all | solution.py:443
  10.8 9.2 %collective-permute-start = (bf16[128,128]{1,0:T(8,128)(2,1)}, bf16[128,128]{1,0:T(8,128)(2,1)S(1)}, u32[]{:S(2)}, u32[]{:S(2)}) collective-permute-start(bf16[128,128]{1,0:T(8,128)(2,1)} %get-tuple-element.28), channel_id=1, source_target_pairs={{0,32},{32,0},{64,96},{96,64},{128,160},{160,128},{192,224},{224,1... | collective-permute-start | bytes 98312 | tf_op jit(solution)/shard_map/ppermute | solution.py:432
  10.9 9.2 %collective-permute-start.1 = (bf16[128,128]{1,0:T(8,128)(2,1)}, bf16[128,128]{1,0:T(8,128)(2,1)S(1)}, u32[]{:S(2)}, u32[]{:S(2)}) collective-permute-start(bf16[128,128]{1,0:T(8,128)(2,1)} %get-tuple-element.29), channel_id=1, source_target_pairs={{32,64},{64,32},{96,128},{128,96},{160,192},{192,160},{33,65},{65,... | collective-permute-start | bytes 98312 | tf_op jit(solution)/shard_map/ppermute | solution.py:432
  15.1 5.0 %collective-permute-start.2 = (bf16[128,128]{1,0:T(8,128)(2,1)S(1)}, bf16[128,128]{1,0:T(8,128)(2,1)S(1)}, u32[]{:S(2)}, u32[]{:S(2)}) collective-permute-start(bf16[128,128]{1,0:T(8,128)(2,1)S(1)} %copy-done.7), channel_id=1, source_target_pairs={{0,1},{1,0},{2,3},{3,2},{4,5},{5,4},{6,7},{7,6},{8,9},{9,8},{10,11... | collective-permute-start | bytes 98312 | tf_op jit(solution)/shard_map/ppermute | solution.py:432
  17.0 7.3 %collective-permute-start.3 = (bf16[128,128]{1,0:T(8,128)(2,1)S(1)}, bf16[128,128]{1,0:T(8,128)(2,1)S(1)}, u32[]{:S(2)}, u32[]{:S(2)}) collective-permute-start(bf16[128,128]{1,0:T(8,128)(2,1)S(1)} %copy-done.5), channel_id=1, source_target_pairs={{1,2},{2,1},{3,4},{4,3},{5,6},{6,5},{7,8},{8,7},{9,10},{10,9},{11,... | collective-permute-start | bytes 98312 | tf_op jit(solution)/shard_map/ppermute | solution.py:432
  20.0 5.2 %copy-start = (bf16[128,128]{1,0:T(8,128)(2,1)}, bf16[128,128]{1,0:T(8,128)(2,1)S(1)}, u32[]{:S(2)}) copy-start(bf16[128,128]{1,0:T(8,128)(2,1)S(1)} %collective-permute-done.refs_1_) | copy-start | bytes 98308
  20.1 5.2 %copy-start.1 = (bf16[128,128]{1,0:T(8,128)(2,1)}, bf16[128,128]{1,0:T(8,128)(2,1)S(1)}, u32[]{:S(2)}) copy-start(bf16[128,128]{1,0:T(8,128)(2,1)S(1)} %collective-permute-done.1.refs_2_) | copy-start | bytes 98308
  20.1 5.2 %copy-start.2 = (bf16[128,128]{1,0:T(8,128)(2,1)}, bf16[128,128]{1,0:T(8,128)(2,1)S(1)}, u32[]{:S(2)}) copy-start(bf16[128,128]{1,0:T(8,128)(2,1)S(1)} %collective-permute-done.2.refs_3_) | copy-start | bytes 98308
  24.3 1.0 %copy-start.4 = (bf16[128,128]{1,0:T(8,128)(2,1)}, bf16[128,128]{1,0:T(8,128)(2,1)S(1)}, u32[]{:S(2)}) copy-start(bf16[128,128]{1,0:T(8,128)(2,1)S(1)} %collective-permute-done.3.refs_4_) | copy-start | bytes 98308
  25.3 21.1 %all-to-all-start.1 = ((bf16[32,80,128]{2,1,0:T(8,128)(2,1)}), bf16[32,80,128]{2,1,0:T(8,128)(2,1)}, u32[]{:S(2)}, u32[]{:S(2)}) async-start(bf16[32,80,128]{2,1,0:T(8,128)(2,1)} %middle.1), calls=%async_computation.1 | async-start | bytes 1310720 | tf_op jit(solution)/shard_map/all_to_all | solution.py:443
  50.6 8.8 %collective-permute-start.4 = (bf16[128,128]{1,0:T(8,128)(2,1)}, bf16[128,128]{1,0:T(8,128)(2,1)S(1)}, u32[]{:S(2)}, u32[]{:S(2)}) collective-permute-start(bf16[128,128]{1,0:T(8,128)(2,1)} %get-tuple-element.43), channel_id=1, source_target_pairs={{0,32},{32,0},{64,96},{96,64},{128,160},{160,128},{192,224},{224,1... | collective-permute-start | bytes 98312 | tf_op jit(solution)/shard_map/ppermute | solution.py:432
  50.6 8.9 %collective-permute-start.5 = (bf16[128,128]{1,0:T(8,128)(2,1)}, bf16[128,128]{1,0:T(8,128)(2,1)S(1)}, u32[]{:S(2)}, u32[]{:S(2)}) collective-permute-start(bf16[128,128]{1,0:T(8,128)(2,1)} %get-tuple-element.44), channel_id=1, source_target_pairs={{32,64},{64,32},{96,128},{128,96},{160,192},{192,160},{33,65},{65,... | collective-permute-start | bytes 98312 | tf_op jit(solution)/shard_map/ppermute | solution.py:432
  55.2 4.3 %collective-permute-start.6 = (bf16[128,128]{1,0:T(8,128)(2,1)}, bf16[128,128]{1,0:T(8,128)(2,1)S(1)}, u32[]{:S(2)}, u32[]{:S(2)}) collective-permute-start(bf16[128,128]{1,0:T(8,128)(2,1)} %get-tuple-element.45), channel_id=1, source_target_pairs={{0,1},{1,0},{2,3},{3,2},{4,5},{5,4},{6,7},{7,6},{8,9},{9,8},{10,11... | collective-permute-start | bytes 98312 | tf_op jit(solution)/shard_map/ppermute | solution.py:432
  56.2 7.5 %collective-permute-start.7 = (bf16[128,128]{1,0:T(8,128)(2,1)}, bf16[128,128]{1,0:T(8,128)(2,1)S(1)}, u32[]{:S(2)}, u32[]{:S(2)}) collective-permute-start(bf16[128,128]{1,0:T(8,128)(2,1)} %get-tuple-element.46), channel_id=1, source_target_pairs={{1,2},{2,1},{3,4},{4,3},{5,6},{6,5},{7,8},{8,7},{9,10},{10,9},{11,... | collective-permute-start | bytes 98312 | tf_op jit(solution)/shard_map/ppermute | solution.py:432
  59.4 4.3 %copy-start.3 = (bf16[128,128]{1,0:T(8,128)(2,1)}, bf16[128,128]{1,0:T(8,128)(2,1)S(1)}, u32[]{:S(2)}) copy-start(bf16[128,128]{1,0:T(8,128)(2,1)S(1)} %collective-permute-done.4.refs_1_) | copy-start | bytes 98308
  59.5 4.3 %copy-start.6 = (bf16[128,128]{1,0:T(8,128)(2,1)}, bf16[128,128]{1,0:T(8,128)(2,1)S(1)}, u32[]{:S(2)}) copy-start(bf16[128,128]{1,0:T(8,128)(2,1)S(1)} %collective-permute-done.5.refs_2_) | copy-start | bytes 98308
  59.5 4.3 %copy-start.8 = (bf16[128,128]{1,0:T(8,128)(2,1)}, bf16[128,128]{1,0:T(8,128)(2,1)S(1)}, u32[]{:S(2)}) copy-start(bf16[128,128]{1,0:T(8,128)(2,1)S(1)} %collective-permute-done.6.refs_3_) | copy-start | bytes 98308
  63.8 0.6 copy-start.9

commit v3 on v2

--- a/solution.py
+++ b/solution.py
@@ -177,18 +177,32 @@
     return fresh, dot(turned, fresh_two)
 
 
-def edge_kernel(layer, last, *refs):
-    nodes_ref, *refs = refs
-    halo, refs = refs[:4], refs[4:]
-    (send_hbm, recv_hbm, receivers_ref, edges_hbm, w_in_ref, w_out_ref, bias_ref, gain_ref), refs = (
-        refs[:8],
-        refs[8:],
-    )
-    if last:
-        node_refs, refs = refs[:7], refs[7:]
+def slice_shape(arg):
+    if arg.ndim != 3 or arg.shape[0] != LAYERS:
+        return arg.shape
+    return (1, *arg.shape[1:])
+
+
+def fetches(sources, kept, sems, layer):
+    copies = []
+    for k, (source, ref) in enumerate(zip(sources, kept)):
+        if source.shape != ref.shape:
+            source = source.at[pl.ds(layer, 1)]
+        copies.append(pltpu.make_async_copy(source, ref, sems.at[k]))
+    return copies
+
+
+def edge_kernel(layer, last, count, *refs):
+    args, refs = refs[:count], refs[count:]
+    send_hbm, recv_hbm, edges_hbm, *small = args
     fresh_hbm, node_side, *refs = refs
     send_table, recv_table, acc, w_two, even_pre, odd_pre, *refs = refs
-    send_col, recv_col, edges_ref, fresh_buf, in_sems, out_sems = refs
+    send_col, recv_col, edges_ref, fresh_buf, in_sems, out_sems, small_sems, *kept = refs
+    nodes_ref, *rest = kept
+    halo, rest = rest[:4], rest[4:]
+    receivers_ref, w_in_ref, w_out_ref, bias_ref, gain_ref, *node_refs = rest
+    early = len(kept) - len(node_refs)
+    small_copies = fetches(small, kept, small_sems, layer)
     recv_half = nodes_ref.shape[0] // 2
     steps = edges_ref.shape[0] // TILE
     per = TILE // W
@@ -210,9 +224,15 @@
         at = strip(i)
         return pltpu.make_async_copy(fresh_buf.at[at], fresh_hbm.at[at], out_sems.at[i])
 
-    for i in range(steps):
+    for copy in small_copies[:early] + in_copies(0):
+        copy.start()
+    for i in range(1, steps):
         for copy in in_copies(i):
             copy.start()
+    for copy in small_copies[early:]:
+        copy.start()
+    for copy in small_copies[:early]:
+        copy.wait()
 
     project(nodes_ref[...], [h[...] for h in halo], w_in_ref[0], send_table, recv_table)
     two, b_centred = centred_weights(w_out_ref[0], bias_ref[1, layer : layer + 1])
@@ -240,8 +260,8 @@
 
     def both(i, now, later):
         arrive(i + 1)
+        fresh, added = tail_of(i, now[...])
         pre = pre_of(i + 1)
-        fresh, added = tail_of(i, now[...])
         later[...] = pre
         acc[...] += added
         fresh_buf[strip(i)] = fresh
@@ -263,6 +283,8 @@
     sums = acc[...] + added
     summed = jnp.concatenate([sums[:, :W], sums[:, W:]], axis=0).astype(BF)
     if last:
+        for copy in small_copies[early:]:
+            copy.wait()
         context_ref, pooled_ref, *weights = node_refs
         node_side[...] = node_update(
             layer, nodes_ref[...], summed, context_ref[...], pooled_ref[...], *weights
@@ -295,18 +317,14 @@
     node_count, edge_count = nodes.shape[0], edges.shape[0]
     half, ext_half = node_count // 2, (node_count + 4 * W) // 2
     flops = 2 * edge_count * W * (2 * ext_half + 4 * half + 8 * W)
-    args = [nodes, *halo, send_col, recv_col, receivers, edges, *weights, *node_args]
-    specs = [of_layer(arg, layer) for arg in args]
-    for k in (1, 2, 3, 4):
-        specs[k] = pl.BlockSpec(memory_space=VM)
-    for k in (5, 6, 8):
-        specs[k] = pl.BlockSpec(memory_space=pltpu.HBM)
+    small = [nodes, *halo, receivers, *weights, *node_args]
+    args = [send_col, recv_col, edges, *small]
     steps = edge_count // TILE
     return pl.pallas_call(
-        functools.partial(edge_kernel, layer, last),
+        functools.partial(edge_kernel, layer, last, len(args)),
         grid=(1,),
-        in_specs=specs,
-        out_specs=[pl.BlockSpec(memory_space=pltpu.HBM), whole(nodes)],
+        in_specs=[pl.BlockSpec(memory_space=pl.ANY)] * len(args),
+        out_specs=[pl.BlockSpec(memory_space=pl.ANY), whole(nodes)],
         out_shape=[
             jax.ShapeDtypeStruct(edges.shape, BF),
             jax.ShapeDtypeStruct(nodes.shape, BF),
@@ -324,6 +342,8 @@
             VM(edges.shape, BF),
             pltpu.SemaphoreType.DMA((3, steps)),
             pltpu.SemaphoreType.DMA((steps,)),
+            pltpu.SemaphoreType.DMA((len(small),)),
+            *[VM(slice_shape(v), v.dtype) for v in small],
         ],
         compiler_params=params(),
         cost_estimate=pl.CostEstimate(

time: 76.3 us -> 75 us (0.983)
  Pallas kernels: 32.4 us -> 31.1 us
    pallas_call x2, Pallas kernels: 21.8 us -> 20.5 us  [edge_step(): pl.pallas_call(functools.partial(edge_kernel, layer, last, len(args)), gr...]
where the time goes in v3:
time: 75 us; the launch traced here: 74.5 us
  starting transfers between devices  33.2 us (44%)
  Pallas kernels  31.1 us (41%)
  waiting for transfers between devices  8.52 us (11%)
  between operations  0.99 us (1%)
    pallas_call x2, Pallas kernels, edge_step(): pl.pallas_call(functools.partial(edge_kernel, layer, last, len(args)), gr...  20.5 us
    ppermute x8, starting transfers between devices, exchanged(): return lax.ppermute(block, axis, pairs)  18 us
    all_to_all x2, starting transfers between devices, to_everyone(): return lax.all_to_all(copies, axis, split_axis=0, concat_axis=0, tiled=True)  15.2 us
    ppermute x8, waiting for transfers between devices, exchanged(): return lax.ppermute(block, axis, pairs)  8.51 us
    pallas_call x1, Pallas kernels, local(): pl.pallas_call(first_node_kernel, grid=(1,), in_specs=[of_layer(v, 0) for...  4.17 us
    pallas_call x1, Pallas kernels, local(): pl.pallas_call(prepare_kernel, out_shape=[column(edge_count), column(edge...  3.46 us
    pallas_call x1, Pallas kernels, local(): pl.pallas_call(start_kernel, out_shape=[jax.ShapeDtypeStruct((n_row, 16,...  2.06 us
  transfers between devices with their start and end apart: 10, of which 2 were waited for; matrix products, arithmetic and copies ran while one was open for 0% of the time, Pallas kernels for 18%

profile of v3, /device:TPU:39, one launch (start us, length us, event | category | flops | bytes accessed | tf_op | source)
XLA Modules:
  0.0 74.5 jit_solution(547177359180440547)
XLA Ops:
  0.6 2.1 %start.1 = (bf16[8,16,128]{2,1,0:T(8,128)(2,1)}, s16[512,128]{1,0:T(8,128)(2,1)}, bf16[128,128]{1,0:T(8,128)(2,1)}, bf16[128,128]{1,0:T(8,128)(2,1)}, bf16[128,1...) custom-call(bf16[1024,128]{1,0:T(8,128)(2,1)} %nodes_ref.3, s32[1,4,128]{2,1,0:T(4,128)} %send_ref.1, bf16[8,128]{1,0:T(8,128)(2,1)} %context_ref.1), custom_call_target="tpu_custom_call" | custom-call | tf_op jit(solution)/shard_map/start/pallas_call | solution.py:490
  2.7 8.1 %all-to-all-start = ((bf16[8,16,128]{2,1,0:T(8,128)(2,1)}), bf16[8,16,128]{2,1,0:T(8,128)(2,1)S(1)}, u32[]{:S(2)}, u32[]{:S(2)}) async-start(bf16[8,16,128]{2,1,0:T(8,128)(2,1)} %get-tuple-element.29), calls=%async_computation | async-start | bytes 65536 | tf_op jit(solution)/shard_map/all_to_all | solution.py:463
  10.8 0.0 collective-permute-start
  10.9 4.2 %collective-permute-start.1 = (bf16[128,128]{1,0:T(8,128)(2,1)}, bf16[128,128]{1,0:T(8,128)(2,1)S(1)}, u32[]{:S(2)}, u32[]{:S(2)}) collective-permute-start(bf16[128,128]{1,0:T(8,128)(2,1)} %get-tuple-element.31), channel_id=1, source_target_pairs={{32,64},{64,32},{96,128},{128,96},{160,192},{192,160},{33,65},{65,... | collective-permute-start | bytes 98312 | tf_op jit(solution)/shard_map/ppermute | solution.py:452
  15.1 0.0 copy-done.7
  15.1 1.9 %collective-permute-start.2 = (bf16[128,128]{1,0:T(8,128)(2,1)S(1)}, bf16[128,128]{1,0:T(8,128)(2,1)S(1)}, u32[]{:S(2)}, u32[]{:S(2)}) collective-permute-start(bf16[128,128]{1,0:T(8,128)(2,1)S(1)} %copy-done.7), channel_id=1, source_target_pairs={{0,1},{1,0},{2,3},{3,2},{4,5},{5,4},{6,7},{7,6},{8,9},{9,8},{10,11... | collective-permute-start | bytes 98312 | tf_op jit(solution)/shard_map/ppermute | solution.py:452
  17.0 0.0 copy-done.5
  17.0 3.0 %collective-permute-start.3 = (bf16[128,128]{1,0:T(8,128)(2,1)S(1)}, bf16[128,128]{1,0:T(8,128)(2,1)S(1)}, u32[]{:S(2)}, u32[]{:S(2)}) collective-permute-start(bf16[128,128]{1,0:T(8,128)(2,1)S(1)} %copy-done.5), channel_id=1, source_target_pairs={{1,2},{2,1},{3,4},{4,3},{5,6},{6,5},{7,8},{8,7},{9,10},{10,9},{11,... | collective-permute-start | bytes 98312 | tf_op jit(solution)/shard_map/ppermute | solution.py:452
  20.0 0.0 collective-permute-done.refs_4_
  20.0 0.0 copy-start
  20.1 0.0 collective-permute-done.1.refs_5_
  20.1 0.0 collective-permute-done.2.refs_6_
  20.1 4.2 %collective-permute-done.3.refs_7_ = bf16[128,128]{1,0:T(8,128)(2,1)S(1)} collective-permute-done((bf16[128,128]{1,0:T(8,128)(2,1)S(1)}, bf16[128,128]{1,0:T(8,128)(2,1)S(1)}, u32[]{:S(2)}, u32[]{:S(2)}) %collective-permute-start.3) | collective-permute-done | bytes 32800 | tf_op jit(solution)/shard_map/ppermute | solution.py:452
  24.3 0.0 all-to-all-done.got_ref
  24.3 0.9 %middle.1 = bf16[32,80,128]{2,1,0:T(8,128)(2,1)} custom-call(bf16[8,16,128]{2,1,0:T(8,128)(2,1)S(1)} %all-to-all-done.got_ref), custom_call_target="tpu_custom_call" | custom-call | tf_op jit(solution)/shard_map/middle/pallas_call | solution.py:508
  25.3 7.1 %all-to-all-start.1 = ((bf16[32,80,128]{2,1,0:T(8,128)(2,1)}), bf16[32,80,128]{2,1,0:T(8,128)(2,1)}, u32[]{:S(2)}, u32[]{:S(2)}) async-start(bf16[32,80,128]{2,1,0:T(8,128)(2,1)} %middle.1), calls=%async_computation.1 | async-start | bytes 1310720 | tf_op jit(solution)/shard_map/all_to_all | solution.py:463
  32.4 3.5 %prepare.1 = (s16[4096,128]{1,0:T(8,128)(2,1)}, s16[4096,128]{1,0:T(8,128)(2,1)}, s16[1024,128]{1,0:T(8,128)(2,1)}) custom-call(s32[32,128]{1,0:T(8,128)} %bitcast.7, s32[32,128]{1,0:T(8,128)} %bitcast.8, s32[8,128]{1,0:T(8,128)} %bitcast.11), custom_call_target="tpu_custom_call" | custom-call | flops 536870912 | bytes 2097152 | tf_op jit(solution)/shard_map/prepare/pallas_call | solution.py:498
  35.8 10.2 %shard_map.167 = (bf16[4096,128]{1,0:T(8,128)(2,1)}, bf16[1024,128]{1,0:T(8,128)(2,1)}) custom-call(s16[4096,128]{1,0:T(8,128)(2,1)} %get-tuple-element.27.refs_0_, s16[4096,128]{1,0:T(8,128)(2,1)} %get-tuple-element.28.refs_1_, bf16[4096,128]{1,0:T(8,128)(2,1)} %refs_2_.1, bf16[1024,128]{1,0:T(8,128)(2,1)} %nodes_ref.3, bf16[128,128]{1,0:T(8,128)(2,1)} %copy-done, ...), custom_call_target="tpu_custom_call" | custom-call | flops 4831838208 | bytes 2097152 | tf_op jit(solution)/shard_map/pallas_call | solution.py:323
  46.0 0.0 all-to-all-done.1.table_ref
  46.1 4.2 %nodes_0.1 = (bf16[1024,128]{1,0:T(8,128)(2,1)}, bf16[1024,128]{1,0:T(8,128)(2,1)}, f32[1,128]{1,0:T(1,128)}, bf16[128,128]{1,0:T(8,128)(2,1)}, bf16[128,128]{1,...) custom-call(bf16[1024,128]{1,0:T(8,128)(2,1)} %nodes_ref.3, ...), custom_call_target="tpu_custom_call" | custom-call | tf_op jit(solution)/shard_map/nodes_0/pallas_call | solution.py:527
  50.2 0.0 collective-permute-start.4
  50.2 4.6 %collective-permute-start.5 = (bf16[128,128]{1,0:T(8,128)(2,1)}, bf16[128,128]{1,0:T(8,128)(2,1)S(1)}, u32[]{:S(2)}, u32[]{:S(2)}) collective-permute-start(bf16[128,128]{1,0:T(8,128)(2,1)} %get-tuple-element.45), channel_id=1, source_target_pairs={{32,64},{64,32},{96,128},{128,96},{160,192},{192,160},{33,65},{65,... | collective-permute-start | bytes 98312 | tf_op jit(solution)/shard_map/ppermute | solution.py:452
  54.8 1.0 %collective-permute-start.6 = (bf16[128,128]{1,0:T(8,128)(2,1)}, bf16[128,128]{1,0:T(8,128)(2,1)S(1)}, u32[]{:S(2)}, u32[]{:S(2)}) collective-permute-start(bf16[128,128]{1,0:T(8,128)(2,1)} %get-tuple-element.46), channel_id=1, source_target_pairs={{0,1},{1,0},{2,3},{3,2},{4,5},{5,4},{6,7},{7,6},{8,9},{9,8},{10,11... | collective-permute-start | bytes 98312 | tf_op jit(solution)/shard_map/ppermute | solution.py:452
  55.8 3.2 %collective-permute-start.7 = (bf16[128,128]{1,0:T(8,128)(2,1)}, bf16[128,128]{1,0:T(8,128)(2,1)S(1)}, u32[]{:S(2)}, u32[]{:S(2)}) collective-permute-start(bf16[128,128]{1,0:T(8,128)(2,1)} %get-tuple-element.47), channel_id=1, source_target_pairs={{1,2},{2,1},{3,4},{4,3},{5,6},{6,5},{7,8},{8,7},{9,10},{10,9},{11,... | collective-permute-start | bytes 98312 | tf_op jit(solution)/shard_map/ppermute | solution.py:452
  59.1 0.0 collective-permute-done.4.refs_4_
  59.1 0.0 collective-permute-done.5.refs_5_
  59.1 0.0 copy-start.6
  59.1 0.0 collective-permute-done.6.refs_6_
  59.1 4.3 %collective-permute-done.7.refs_7_ = bf16[128,128]{1,0:T(8,128)(2,1)S(1)} collective-permute-done((bf16[128,128]{1,0:T(8,128)(2,1)}, bf16[128,128]{1,0:T(8,128)(2,1)S(1)}, u32[]{:S(2)}, u32[]{:S(2)}) %collective-permute-start.7) | collective-permute-done | bytes 32800 | tf_op jit(solution)/shard_map/ppermute | solution.py:452
  63.4 0.0 copy-done.6
  63.4 0.6 copy-done.9
  64.0 10.3 %shard_map.168 = (bf16[4096,128]{1,0:T(8,128)(2,1)}, bf16[1024,128]{1,0:T(8,128)(2,1)}) custom-call(s16[4096,128]{1,0:T(8,128)(2,1)} %get-tuple-element.27.refs_0_, s16[4096,128]{1,0:T(8,128)(2,1)} %get-tuple-element.28.refs_1_, bf16[4096,128]{1,0:T(8,128)(2,1)} %get-tuple-element.38.refs_2_, bf16[1024,128]{1,0:T(8,128)(2,1)} %get-tuple-element.43.refs_3_, ...), custom_call_target="tpu_custom_call" | custom-call | flops 4831838208 | bytes 2097152 | tf_op jit(solution)/shard_map/pallas_call | solution.py:323
  (14 shorter events, 0.0 us)
Async XLA Ops:
  2.7 12.4 %copy-start.7 = (bf16[128,128]{1,0:T(8,128)(2,1)S(1)}, bf16[128,128]{1,0:T(8,128)(2,1)}, u32[]{:S(2)}) copy-start(bf16[128,128]{1,0:T(8,128)(2,1)} %get-tuple-element.32) | copy-start | bytes 98308
  2.7 14.3 %copy-start.5 = (bf16[128,128]{1,0:T(8,128)(2,1)S(1)}, bf16[128,128]{1,0:T(8,128)(2,1)}, u32[]{:S(2)}) copy-start(bf16[128,128]{1,0:T(8,128)(2,1)} %get-tuple-element.33) | copy-start | bytes 98308
  2.7 21.6 %all-to-all-start = ((bf16[8,16,128]{2,1,0:T(8,128)(2,1)}), bf16[8,16,128]{2,1,0:T(8,128)(2,1)S(1)}, u32[]{:S(2)}, u32[]{:S(2)}) async-start(bf16[8,16,128]{2,1,0:T(8,128)(2,1)} %get-tuple-element.29), calls=%async_computation | async-start | bytes 65536 | tf_op jit(solution)/shard_map/all_to_all | solution.py:463
  10.8 9.2 %collective-permute-start = (bf16[128,128]{1,0:T(8,128)(2,1)}, bf16[128,128]{1,0:T(8,128)(2,1)S(1)}, u32[]{:S(2)}, u32[]{:S(2)}) collective-permute-start(bf16[128,128]{1,0:T(8,128)(2,1)} %get-tuple-element.30), channel_id=1, source_target_pairs={{0,32},{32,0},{64,96},{96,64},{128,160},{160,128},{192,224},{224,1... | collective-permute-start | bytes 98312 | tf_op jit(solution)/shard_map/ppermute | solution.py:452
  10.9 9.2 %collective-permute-start.1 = (bf16[128,128]{1,0:T(8,128)(2,1)}, bf16[128,128]{1,0:T(8,128)(2,1)S(1)}, u32[]{:S(2)}, u32[]{:S(2)}) collective-permute-start(bf16[128,128]{1,0:T(8,128)(2,1)} %get-tuple-element.31), channel_id=1, source_target_pairs={{32,64},{64,32},{96,128},{128,96},{160,192},{192,160},{33,65},{65,... | collective-permute-start | bytes 98312 | tf_op jit(solution)/shard_map/ppermute | solution.py:452
  15.1 5.0 %collective-permute-start.2 = (bf16[128,128]{1,0:T(8,128)(2,1)S(1)}, bf16[128,128]{1,0:T(8,128)(2,1)S(1)}, u32[]{:S(2)}, u32[]{:S(2)}) collective-permute-start(bf16[128,128]{1,0:T(8,128)(2,1)S(1)} %copy-done.7), channel_id=1, source_target_pairs={{0,1},{1,0},{2,3},{3,2},{4,5},{5,4},{6,7},{7,6},{8,9},{9,8},{10,11... | collective-permute-start | bytes 98312 | tf_op jit(solution)/shard_map/ppermute | solution.py:452
  17.0 7.3 %collective-permute-start.3 = (bf16[128,128]{1,0:T(8,128)(2,1)S(1)}, bf16[128,128]{1,0:T(8,128)(2,1)S(1)}, u32[]{:S(2)}, u32[]{:S(2)}) collective-permute-start(bf16[128,128]{1,0:T(8,128)(2,1)S(1)} %copy-done.5), channel_id=1, source_target_pairs={{1,2},{2,1},{3,4},{4,3},{5,6},{6,5},{7,8},{8,7},{9,10},{10,9},{11,... | collective-permute-start | bytes 98312 | tf_op jit(solution)/shard_map/ppermute | solution.py:452
  20.0 5.2 %copy-start = (bf16[128,128]{1,0:T(8,128)(2,1)}, bf16[128,128]{1,0:T(8,128)(2,1)S(1)}, u32[]{:S(2)}) copy-start(bf16[128,128]{1,0:T(8,128)(2,1)S(1)} %collective-permute-done.refs_4_) | copy-start | bytes 98308
  20.1 5.2 %copy-start.1 = (bf16[128,128]{1,0:T(8,128)(2,1)}, bf16[128,128]{1,0:T(8,128)(2,1)S(1)}, u32[]{:S(2)}) copy-start(bf16[128,128]{1,0:T(8,128)(2,1)S(1)} %collective-permute-done.1.refs_5_) | copy-start | bytes 98308
  20.1 5.2 %copy-start.2 = (bf16[128,128]{1,0:T(8,128)(2,1)}, bf16[128,128]{1,0:T(8,128)(2,1)S(1)}, u32[]{:S(2)}) copy-start(bf16[128,128]{1,0:T(8,128)(2,1)S(1)} %collective-permute-done.2.refs_6_) | copy-start | bytes 98308
  24.3 1.0 %copy-start.4 = (bf16[128,128]{1,0:T(8,128)(2,1)}, bf16[128,128]{1,0:T(8,128)(2,1)S(1)}, u32[]{:S(2)}) copy-start(bf16[128,128]{1,0:T(8,128)(2,1)S(1)} %collective-permute-done.3.refs_7_) | copy-start | bytes 98308
  25.3 20.8 %all-to-all-start.1 = ((bf16[32,80,128]{2,1,0:T(8,128)(2,1)}), bf16[32,80,128]{2,1,0:T(8,128)(2,1)}, u32[]{:S(2)}, u32[]{:S(2)}) async-start(bf16[32,80,128]{2,1,0:T(8,128)(2,1)} %middle.1), calls=%async_computation.1 | async-start | bytes 1310720 | tf_op jit(solution)/shard_map/all_to_all | solution.py:463
  50.2 8.8 %collective-permute-start.4 = (bf16[128,128]{1,0:T(8,128)(2,1)}, bf16[128,128]{1,0:T(8,128)(2,1)S(1)}, u32[]{:S(2)}, u32[]{:S(2)}) collective-permute-start(bf16[128,128]{1,0:T(8,128)(2,1)} %get-tuple-element.44), channel_id=1, source_target_pairs={{0,32},{32,0},{64,96},{96,64},{128,160},{160,128},{192,224},{224,1... | collective-permute-start | bytes 98312 | tf_op jit(solution)/shard_map/ppermute | solution.py:452
  50.2 8.9 %collective-permute-start.5 = (bf16[128,128]{1,0:T(8,128)(2,1)}, bf16[128,128]{1,0:T(8,128)(2,1)S(1)}, u32[]{:S(2)}, u32[]{:S(2)}) collective-permute-start(bf16[128,128]{1,0:T(8,128)(2,1)} %get-tuple-element.45), channel_id=1, source_target_pairs={{32,64},{64,32},{96,128},{128,96},{160,192},{192,160},{33,65},{65,... | collective-permute-start | bytes 98312 | tf_op jit(solution)/shard_map/ppermute | solution.py:452
  54.8 4.3 %collective-permute-start.6 = (bf16[128,128]{1,0:T(8,128)(2,1)}, bf16[128,128]{1,0:T(8,128)(2,1)S(1)}, u32[]{:S(2)}, u32[]{:S(2)}) collective-permute-start(bf16[128,128]{1,0:T(8,128)(2,1)} %get-tuple-element.46), channel_id=1, source_target_pairs={{0,1},{1,0},{2,3},{3,2},{4,5},{5,4},{6,7},{7,6},{8,9},{9,8},{10,11... | collective-permute-start | bytes 98312 | tf_op jit(solution)/shard_map/ppermute | solution.py:452
  55.8 7.5 %collective-permute-start.7 = (bf16[128,128]{1,0:T(8,128)(2,1)}, bf16[128,128]{1,0:T(8,128)(2,1)S(1)}, u32[]{:S(2)}, u32[]{:S(2)}) collective-permute-start(bf16[128,128]{1,0:T(8,128)(2,1)} %get-tuple-element.47), channel_id=1, source_target_pairs={{1,2},{2,1},{3,4},{4,3},{5,6},{6,5},{7,8},{8,7},{9,10},{10,9},{11,... | collective-permute-start | bytes 98312 | tf_op jit(solution)/shard_map/ppermute | solution.py:452
  59.1 4.3 %copy-start.3 = (bf16[128,128]{1,0:T(8,128)(2,1)}, bf16[128,128]{1,0:T(8,128)(2,1)S(1)}, u32[]{:S(2)}) copy-start(bf16[128,128]{1,0:T(8,128)(2,1)S(1)} %collective-permute-done.4.refs_4_) | copy-start | bytes 98308
  59.1 4.3 %copy-start.6 = (bf16[128,128]{1,0:T(8,128)(2,1)}, bf16[128,128]{1,0:T(8,128)(2,1)S(1)}, u32[]{:S(2)}) copy-start(bf16[128,128]{1,0:T(8,128)(2,1)S(1)} %collective-permute-done.5.refs_5_) | copy-start | bytes 98308
  59.1 4.3 %copy-start.8 = (bf16[128,128]{1,0:T(8,128)(2,1)}, bf16[128,128]{1,0:T(8,128)(2,1)S(1)}, u32[]{:S(2)}) copy-start(bf16[128,128]{1,0:T(8,128)(2,1)S(1)} %collective-permute-done.6.refs_6_) | copy-start | bytes 98308
  63.4 0.6 copy-start.9

commit v4 on v3

--- a/solution.py
+++ b/solution.py
@@ -16,6 +16,7 @@
 EPS = 1e-05
 W = 128
 TILE = 1024
+SEND_BITS = 11
 BF = jnp.bfloat16
 F32 = jnp.float32
 VM = pltpu.VMEM
@@ -376,13 +377,14 @@
     senders = jnp.where(senders < node_count, senders, senders ^ flip)
     region = region_ref[...]
     place = ((region >> 3) & 31) * 64 + (region >> 8) * 8 + (region & 7)
-    for values, ref in (
-        (senders, send_col),
-        (receivers_ref[...], recv_col),
-        (place, region_col),
-    ):
-        for k, block in enumerate(columns(values, values.shape[0])):
-            ref[W * k : W * (k + 1)] = block
+    both = jnp.transpose((receivers_ref[...] << SEND_BITS) | senders)
+    for k in range(both.shape[1]):
+        wide = jnp.broadcast_to(both[:, k : k + 1], (W, W))
+        rows = slice(W * k, W * (k + 1))
+        send_col[rows] = (wide & (2**SEND_BITS - 1)).astype(jnp.int16)
+        recv_col[rows] = (wide >> SEND_BITS).astype(jnp.int16)
+    for k, block in enumerate(columns(place, place.shape[0])):
+        region_col[W * k : W * (k + 1)] = block
 
 
 def first_node_kernel(

time: 75 us -> 74.5 us (level)
  no operation moved by 1% of the time
where the time goes in v4:
time: 74.5 us; the launch traced here: 74 us
  starting transfers between devices  33 us (44%)
  Pallas kernels  30.6 us (41%)
  waiting for transfers between devices  8.74 us (12%)
  between operations  0.97 us (1%)
    pallas_call x2, Pallas kernels, edge_step(): pl.pallas_call(functools.partial(edge_kernel, layer, last, len(args)), gr...  20.5 us
    ppermute x8, starting transfers between devices, exchanged(): return lax.ppermute(block, axis, pairs)  17.8 us
    all_to_all x2, starting transfers between devices, to_everyone(): return lax.all_to_all(copies, axis, split_axis=0, concat_axis=0, tiled=True)  15.2 us
    ppermute x8, waiting for transfers between devices, exchanged(): return lax.ppermute(block, axis, pairs)  8.73 us
    pallas_call x1, Pallas kernels, local(): pl.pallas_call(first_node_kernel, grid=(1,), in_specs=[of_layer(v, 0) for...  4.17 us
    pallas_call x1, Pallas kernels, local(): pl.pallas_call(prepare_kernel, out_shape=[column(edge_count), column(edge...  2.98 us
    pallas_call x1, Pallas kernels, local(): pl.pallas_call(start_kernel, out_shape=[jax.ShapeDtypeStruct((n_row, 16,...  2.06 us
  transfers between devices with their start and end apart: 10, of which 2 were waited for; matrix products, arithmetic and copies ran while one was open for 0% of the time, Pallas kernels for 18%

profile of v4, /device:TPU:39, one launch (start us, length us, event | category | flops | bytes accessed | tf_op | source)
XLA Modules:
  0.0 74.0 jit_solution(9084808182984050382)
XLA Ops:
  0.6 2.1 %start.1 = (bf16[8,16,128]{2,1,0:T(8,128)(2,1)}, s16[512,128]{1,0:T(8,128)(2,1)}, bf16[128,128]{1,0:T(8,128)(2,1)}, bf16[128,128]{1,0:T(8,128)(2,1)}, bf16[128,1...) custom-call(bf16[1024,128]{1,0:T(8,128)(2,1)} %nodes_ref.3, s32[1,4,128]{2,1,0:T(4,128)} %send_ref.1, bf16[8,128]{1,0:T(8,128)(2,1)} %context_ref.1), custom_call_target="tpu_custom_call" | custom-call | tf_op jit(solution)/shard_map/start/pallas_call | solution.py:492
  2.7 8.1 %all-to-all-start = ((bf16[8,16,128]{2,1,0:T(8,128)(2,1)}), bf16[8,16,128]{2,1,0:T(8,128)(2,1)S(1)}, u32[]{:S(2)}, u32[]{:S(2)}) async-start(bf16[8,16,128]{2,1,0:T(8,128)(2,1)} %get-tuple-element.29), calls=%async_computation | async-start | bytes 65536 | tf_op jit(solution)/shard_map/all_to_all | solution.py:465
  10.8 0.0 collective-permute-start
  10.9 4.2 %collective-permute-start.1 = (bf16[128,128]{1,0:T(8,128)(2,1)}, bf16[128,128]{1,0:T(8,128)(2,1)S(1)}, u32[]{:S(2)}, u32[]{:S(2)}) collective-permute-start(bf16[128,128]{1,0:T(8,128)(2,1)} %get-tuple-element.31), channel_id=1, source_target_pairs={{32,64},{64,32},{96,128},{128,96},{160,192},{192,160},{33,65},{65,... | collective-permute-start | bytes 98312 | tf_op jit(solution)/shard_map/ppermute | solution.py:454
  15.1 0.0 copy-done.7
  15.1 1.9 %collective-permute-start.2 = (bf16[128,128]{1,0:T(8,128)(2,1)S(1)}, bf16[128,128]{1,0:T(8,128)(2,1)S(1)}, u32[]{:S(2)}, u32[]{:S(2)}) collective-permute-start(bf16[128,128]{1,0:T(8,128)(2,1)S(1)} %copy-done.7), channel_id=1, source_target_pairs={{0,1},{1,0},{2,3},{3,2},{4,5},{5,4},{6,7},{7,6},{8,9},{9,8},{10,11... | collective-permute-start | bytes 98312 | tf_op jit(solution)/shard_map/ppermute | solution.py:454
  17.0 0.0 copy-done.5
  17.0 3.0 %collective-permute-start.3 = (bf16[128,128]{1,0:T(8,128)(2,1)S(1)}, bf16[128,128]{1,0:T(8,128)(2,1)S(1)}, u32[]{:S(2)}, u32[]{:S(2)}) collective-permute-start(bf16[128,128]{1,0:T(8,128)(2,1)S(1)} %copy-done.5), channel_id=1, source_target_pairs={{1,2},{2,1},{3,4},{4,3},{5,6},{6,5},{7,8},{8,7},{9,10},{10,9},{11,... | collective-permute-start | bytes 98312 | tf_op jit(solution)/shard_map/ppermute | solution.py:454
  20.0 0.0 collective-permute-done.refs_4_
  20.0 0.0 copy-start
  20.1 0.0 collective-permute-done.1.refs_5_
  20.1 0.0 collective-permute-done.2.refs_6_
  20.1 4.2 %collective-permute-done.3.refs_7_ = bf16[128,128]{1,0:T(8,128)(2,1)S(1)} collective-permute-done((bf16[128,128]{1,0:T(8,128)(2,1)S(1)}, bf16[128,128]{1,0:T(8,128)(2,1)S(1)}, u32[]{:S(2)}, u32[]{:S(2)}) %collective-permute-start.3) | collective-permute-done | bytes 32800 | tf_op jit(solution)/shard_map/ppermute | solution.py:454
  24.3 0.0 all-to-all-done.got_ref
  24.3 0.9 %middle.1 = bf16[32,80,128]{2,1,0:T(8,128)(2,1)} custom-call(bf16[8,16,128]{2,1,0:T(8,128)(2,1)S(1)} %all-to-all-done.got_ref), custom_call_target="tpu_custom_call" | custom-call | tf_op jit(solution)/shard_map/middle/pallas_call | solution.py:510
  25.3 7.1 %all-to-all-start.1 = ((bf16[32,80,128]{2,1,0:T(8,128)(2,1)}), bf16[32,80,128]{2,1,0:T(8,128)(2,1)}, u32[]{:S(2)}, u32[]{:S(2)}) async-start(bf16[32,80,128]{2,1,0:T(8,128)(2,1)} %middle.1), calls=%async_computation.1 | async-start | bytes 1310720 | tf_op jit(solution)/shard_map/all_to_all | solution.py:465
  32.4 3.0 %prepare.1 = (s16[4096,128]{1,0:T(8,128)(2,1)}, s16[4096,128]{1,0:T(8,128)(2,1)}, s16[1024,128]{1,0:T(8,128)(2,1)}) custom-call(s32[32,128]{1,0:T(8,128)} %bitcast.7, s32[32,128]{1,0:T(8,128)} %bitcast.8, s32[8,128]{1,0:T(8,128)} %bitcast.11), custom_call_target="tpu_custom_call" | custom-call | flops 536870912 | bytes 2097152 | tf_op jit(solution)/shard_map/prepare/pallas_call | solution.py:500
  35.4 10.2 %shard_map.167 = (bf16[4096,128]{1,0:T(8,128)(2,1)}, bf16[1024,128]{1,0:T(8,128)(2,1)}) custom-call(s16[4096,128]{1,0:T(8,128)(2,1)} %get-tuple-element.27.refs_0_, s16[4096,128]{1,0:T(8,128)(2,1)} %get-tuple-element.28.refs_1_, bf16[4096,128]{1,0:T(8,128)(2,1)} %refs_2_.1, bf16[1024,128]{1,0:T(8,128)(2,1)} %nodes_ref.3, bf16[128,128]{1,0:T(8,128)(2,1)} %copy-done, ...), custom_call_target="tpu_custom_call" | custom-call | flops 4831838208 | bytes 2097152 | tf_op jit(solution)/shard_map/pallas_call | solution.py:324
  45.6 0.0 all-to-all-done.1.table_ref
  45.6 4.2 %nodes_0.1 = (bf16[1024,128]{1,0:T(8,128)(2,1)}, bf16[1024,128]{1,0:T(8,128)(2,1)}, f32[1,128]{1,0:T(1,128)}, bf16[128,128]{1,0:T(8,128)(2,1)}, bf16[128,128]{1,...) custom-call(bf16[1024,128]{1,0:T(8,128)(2,1)} %nodes_ref.3, ...), custom_call_target="tpu_custom_call" | custom-call | tf_op jit(solution)/shard_map/nodes_0/pallas_call | solution.py:529
  49.7 0.1 collective-permute-start.4
  49.8 4.6 %collective-permute-start.5 = (bf16[128,128]{1,0:T(8,128)(2,1)}, bf16[128,128]{1,0:T(8,128)(2,1)S(1)}, u32[]{:S(2)}, u32[]{:S(2)}) collective-permute-start(bf16[128,128]{1,0:T(8,128)(2,1)} %get-tuple-element.45), channel_id=1, source_target_pairs={{32,64},{64,32},{96,128},{128,96},{160,192},{192,160},{33,65},{65,... | collective-permute-start | bytes 98312 | tf_op jit(solution)/shard_map/ppermute | solution.py:454
  54.4 1.0 %collective-permute-start.6 = (bf16[128,128]{1,0:T(8,128)(2,1)}, bf16[128,128]{1,0:T(8,128)(2,1)S(1)}, u32[]{:S(2)}, u32[]{:S(2)}) collective-permute-start(bf16[128,128]{1,0:T(8,128)(2,1)} %get-tuple-element.46), channel_id=1, source_target_pairs={{0,1},{1,0},{2,3},{3,2},{4,5},{5,4},{6,7},{7,6},{8,9},{9,8},{10,11... | collective-permute-start | bytes 98312 | tf_op jit(solution)/shard_map/ppermute | solution.py:454
  55.4 3.0 %collective-permute-start.7 = (bf16[128,128]{1,0:T(8,128)(2,1)}, bf16[128,128]{1,0:T(8,128)(2,1)S(1)}, u32[]{:S(2)}, u32[]{:S(2)}) collective-permute-start(bf16[128,128]{1,0:T(8,128)(2,1)} %get-tuple-element.47), channel_id=1, source_target_pairs={{1,2},{2,1},{3,4},{4,3},{5,6},{6,5},{7,8},{8,7},{9,10},{10,9},{11,... | collective-permute-start | bytes 98312 | tf_op jit(solution)/shard_map/ppermute | solution.py:454
  58.4 0.0 collective-permute-done.4.refs_4_
  58.4 0.0 collective-permute-done.5.refs_5_
  58.4 0.0 copy-start.6
  58.5 0.0 collective-permute-done.6.refs_6_
  58.5 4.5 %collective-permute-done.7.refs_7_ = bf16[128,128]{1,0:T(8,128)(2,1)S(1)} collective-permute-done((bf16[128,128]{1,0:T(8,128)(2,1)}, bf16[128,128]{1,0:T(8,128)(2,1)S(1)}, u32[]{:S(2)}, u32[]{:S(2)}) %collective-permute-start.7) | collective-permute-done | bytes 32800 | tf_op jit(solution)/shard_map/ppermute | solution.py:454
  63.0 0.0 copy-done.8
  63.0 0.6 copy-done.9
  63.6 10.3 %shard_map.168 = (bf16[4096,128]{1,0:T(8,128)(2,1)}, bf16[1024,128]{1,0:T(8,128)(2,1)}) custom-call(s16[4096,128]{1,0:T(8,128)(2,1)} %get-tuple-element.27.refs_0_, s16[4096,128]{1,0:T(8,128)(2,1)} %get-tuple-element.28.refs_1_, bf16[4096,128]{1,0:T(8,128)(2,1)} %get-tuple-element.38.refs_2_, bf16[1024,128]{1,0:T(8,128)(2,1)} %get-tuple-element.43.refs_3_, ...), custom_call_target="tpu_custom_call" | custom-call | flops 4831838208 | bytes 2097152 | tf_op jit(solution)/shard_map/pallas_call | solution.py:324
  (14 shorter events, 0.0 us)
Async XLA Ops:
  2.7 12.4 %copy-start.7 = (bf16[128,128]{1,0:T(8,128)(2,1)S(1)}, bf16[128,128]{1,0:T(8,128)(2,1)}, u32[]{:S(2)}) copy-start(bf16[128,128]{1,0:T(8,128)(2,1)} %get-tuple-element.32) | copy-start | bytes 98308
  2.7 14.3 %copy-start.5 = (bf16[128,128]{1,0:T(8,128)(2,1)S(1)}, bf16[128,128]{1,0:T(8,128)(2,1)}, u32[]{:S(2)}) copy-start(bf16[128,128]{1,0:T(8,128)(2,1)} %get-tuple-element.33) | copy-start | bytes 98308
  2.7 21.6 %all-to-all-start = ((bf16[8,16,128]{2,1,0:T(8,128)(2,1)}), bf16[8,16,128]{2,1,0:T(8,128)(2,1)S(1)}, u32[]{:S(2)}, u32[]{:S(2)}) async-start(bf16[8,16,128]{2,1,0:T(8,128)(2,1)} %get-tuple-element.29), calls=%async_computation | async-start | bytes 65536 | tf_op jit(solution)/shard_map/all_to_all | solution.py:465
  10.8 9.2 %collective-permute-start = (bf16[128,128]{1,0:T(8,128)(2,1)}, bf16[128,128]{1,0:T(8,128)(2,1)S(1)}, u32[]{:S(2)}, u32[]{:S(2)}) collective-permute-start(bf16[128,128]{1,0:T(8,128)(2,1)} %get-tuple-element.30), channel_id=1, source_target_pairs={{0,32},{32,0},{64,96},{96,64},{128,160},{160,128},{192,224},{224,1... | collective-permute-start | bytes 98312 | tf_op jit(solution)/shard_map/ppermute | solution.py:454
  10.9 9.2 %collective-permute-start.1 = (bf16[128,128]{1,0:T(8,128)(2,1)}, bf16[128,128]{1,0:T(8,128)(2,1)S(1)}, u32[]{:S(2)}, u32[]{:S(2)}) collective-permute-start(bf16[128,128]{1,0:T(8,128)(2,1)} %get-tuple-element.31), channel_id=1, source_target_pairs={{32,64},{64,32},{96,128},{128,96},{160,192},{192,160},{33,65},{65,... | collective-permute-start | bytes 98312 | tf_op jit(solution)/shard_map/ppermute | solution.py:454
  15.1 5.0 %collective-permute-start.2 = (bf16[128,128]{1,0:T(8,128)(2,1)S(1)}, bf16[128,128]{1,0:T(8,128)(2,1)S(1)}, u32[]{:S(2)}, u32[]{:S(2)}) collective-permute-start(bf16[128,128]{1,0:T(8,128)(2,1)S(1)} %copy-done.7), channel_id=1, source_target_pairs={{0,1},{1,0},{2,3},{3,2},{4,5},{5,4},{6,7},{7,6},{8,9},{9,8},{10,11... | collective-permute-start | bytes 98312 | tf_op jit(solution)/shard_map/ppermute | solution.py:454
  17.0 7.3 %collective-permute-start.3 = (bf16[128,128]{1,0:T(8,128)(2,1)S(1)}, bf16[128,128]{1,0:T(8,128)(2,1)S(1)}, u32[]{:S(2)}, u32[]{:S(2)}) collective-permute-start(bf16[128,128]{1,0:T(8,128)(2,1)S(1)} %copy-done.5), channel_id=1, source_target_pairs={{1,2},{2,1},{3,4},{4,3},{5,6},{6,5},{7,8},{8,7},{9,10},{10,9},{11,... | collective-permute-start | bytes 98312 | tf_op jit(solution)/shard_map/ppermute | solution.py:454
  20.0 5.2 %copy-start = (bf16[128,128]{1,0:T(8,128)(2,1)}, bf16[128,128]{1,0:T(8,128)(2,1)S(1)}, u32[]{:S(2)}) copy-start(bf16[128,128]{1,0:T(8,128)(2,1)S(1)} %collective-permute-done.refs_4_) | copy-start | bytes 98308
  20.1 5.2 %copy-start.1 = (bf16[128,128]{1,0:T(8,128)(2,1)}, bf16[128,128]{1,0:T(8,128)(2,1)S(1)}, u32[]{:S(2)}) copy-start(bf16[128,128]{1,0:T(8,128)(2,1)S(1)} %collective-permute-done.1.refs_5_) | copy-start | bytes 98308
  20.1 5.2 %copy-start.2 = (bf16[128,128]{1,0:T(8,128)(2,1)}, bf16[128,128]{1,0:T(8,128)(2,1)S(1)}, u32[]{:S(2)}) copy-start(bf16[128,128]{1,0:T(8,128)(2,1)S(1)} %collective-permute-done.2.refs_6_) | copy-start | bytes 98308
  24.3 1.0 %copy-start.4 = (bf16[128,128]{1,0:T(8,128)(2,1)}, bf16[128,128]{1,0:T(8,128)(2,1)S(1)}, u32[]{:S(2)}) copy-start(bf16[128,128]{1,0:T(8,128)(2,1)S(1)} %collective-permute-done.3.refs_7_) | copy-start | bytes 98308
  25.3 20.3 %all-to-all-start.1 = ((bf16[32,80,128]{2,1,0:T(8,128)(2,1)}), bf16[32,80,128]{2,1,0:T(8,128)(2,1)}, u32[]{:S(2)}, u32[]{:S(2)}) async-start(bf16[32,80,128]{2,1,0:T(8,128)(2,1)} %middle.1), calls=%async_computation.1 | async-start | bytes 1310720 | tf_op jit(solution)/shard_map/all_to_all | solution.py:465
  49.7 8.7 %collective-permute-start.4 = (bf16[128,128]{1,0:T(8,128)(2,1)}, bf16[128,128]{1,0:T(8,128)(2,1)S(1)}, u32[]{:S(2)}, u32[]{:S(2)}) collective-permute-start(bf16[128,128]{1,0:T(8,128)(2,1)} %get-tuple-element.44), channel_id=1, source_target_pairs={{0,32},{32,0},{64,96},{96,64},{128,160},{160,128},{192,224},{224,1... | collective-permute-start | bytes 98312 | tf_op jit(solution)/shard_map/ppermute | solution.py:454
  49.8 8.6 %collective-permute-start.5 = (bf16[128,128]{1,0:T(8,128)(2,1)}, bf16[128,128]{1,0:T(8,128)(2,1)S(1)}, u32[]{:S(2)}, u32[]{:S(2)}) collective-permute-start(bf16[128,128]{1,0:T(8,128)(2,1)} %get-tuple-element.45), channel_id=1, source_target_pairs={{32,64},{64,32},{96,128},{128,96},{160,192},{192,160},{33,65},{65,... | collective-permute-start | bytes 98312 | tf_op jit(solution)/shard_map/ppermute | solution.py:454
  54.4 4.1 %collective-permute-start.6 = (bf16[128,128]{1,0:T(8,128)(2,1)}, bf16[128,128]{1,0:T(8,128)(2,1)S(1)}, u32[]{:S(2)}, u32[]{:S(2)}) collective-permute-start(bf16[128,128]{1,0:T(8,128)(2,1)} %get-tuple-element.46), channel_id=1, source_target_pairs={{0,1},{1,0},{2,3},{3,2},{4,5},{5,4},{6,7},{7,6},{8,9},{9,8},{10,11... | collective-permute-start | bytes 98312 | tf_op jit(solution)/shard_map/ppermute | solution.py:454
  55.4 7.5 %collective-permute-start.7 = (bf16[128,128]{1,0:T(8,128)(2,1)}, bf16[128,128]{1,0:T(8,128)(2,1)S(1)}, u32[]{:S(2)}, u32[]{:S(2)}) collective-permute-start(bf16[128,128]{1,0:T(8,128)(2,1)} %get-tuple-element.47), channel_id=1, source_target_pairs={{1,2},{2,1},{3,4},{4,3},{5,6},{6,5},{7,8},{8,7},{9,10},{10,9},{11,... | collective-permute-start | bytes 98312 | tf_op jit(solution)/shard_map/ppermute | solution.py:454
  58.4 4.5 %copy-start.3 = (bf16[128,128]{1,0:T(8,128)(2,1)}, bf16[128,128]{1,0:T(8,128)(2,1)S(1)}, u32[]{:S(2)}) copy-start(bf16[128,128]{1,0:T(8,128)(2,1)S(1)} %collective-permute-done.4.refs_4_) | copy-start | bytes 98308
  58.4 4.5 %copy-start.6 = (bf16[128,128]{1,0:T(8,128)(2,1)}, bf16[128,128]{1,0:T(8,128)(2,1)S(1)}, u32[]{:S(2)}) copy-start(bf16[128,128]{1,0:T(8,128)(2,1)S(1)} %collective-permute-done.5.refs_5_) | copy-start | bytes 98308
  58.5 4.5 %copy-start.8 = (bf16[128,128]{1,0:T(8,128)(2,1)}, bf16[128,128]{1,0:T(8,128)(2,1)S(1)}, u32[]{:S(2)}) copy-start(bf16[128,128]{1,0:T(8,128)(2,1)S(1)} %collective-permute-done.6.refs_6_) | copy-start | bytes 98308
  63.0 0.6 copy-start.9
